TPU v7x, 32 devices: a whole 2x2x4 slice. The times are simulated.
32 devices in a mesh: gx: 4 (over z), gy: 4 (over x, core), gz: 2 (over y).
Axes of the slice: x: 2, y: 2, z: 4, core: 2. Of those that a mesh axis runs over, the one named last changes fastest.
Arguments:
- inputs: bfloat16 [112, 112, 14, 96], P('gx', 'gy', 'gz'), may hold values from -6 to 6
- d_out: bfloat16 [112, 112, 14, 96], P('gx', 'gy', 'gz'), may hold values from -6 to 6
- layer_norm_gain: float32 [96], replicated, may hold values from 0.1 to 1.9
- layer_norm_bias: float32 [96], replicated, may hold values from -3 to 3
- w_qkv: bfloat16 [96, 288], replicated, may hold values from -0.625 to 0.625
- b_qkv: float32 [288], replicated, may hold values from -3 to 3
- w_proj: bfloat16 [96, 96], replicated, may hold values from -0.625 to 0.625
- rel_bias: float32 [3, 2197], replicated, may hold values from -4 to 240
Outputs:
- d_x: bfloat16 [112, 112, 14, 96], P('gx', 'gy', 'gz')
- g_qkv: float32 [96, 288], replicated
- g_bqkv: float32 [288], replicated
- g_proj: float32 [96, 96], replicated
- g_rel: float32 [3, 2197], replicated
- gain_gradient: float32 [96], replicated
- g_shift: float32 [96], replicated
All inputs are finite; a program needn't handle non-finite values.
Results may differ from a plain program's by a relative error of at most 0.011.
Values may be sent and summed in bfloat16 or wider, within the bound.
No kernel may reach another device: no remote copies, remote signals or barrier semaphores. Data moves between devices by JAX's collectives and lax.ppermute only.
A program may use at most 192 MiB of HBM per device.

v0:
```python
import jax
import jax.numpy as jnp
from jax import lax
from jax.sharding import PartitionSpec as P

WIN = 7
SHIFT = 3


def shifted(block, axis, distance):
    devices = range(lax.axis_size(axis))
    route = [((i - distance) % len(devices), i) for i in devices]
    return lax.ppermute(block, axis, route)


def offset_ones(span):
    first = jnp.arange(span)[:, None, None]
    second = jnp.arange(span)[None, :, None]
    third = jnp.arange(2 * span - 1)[None, None, :]
    return (first - second + span - 1 == third).astype(jnp.float32)


def expand_table(table, span):
    exact = lax.Precision.HIGHEST
    ones = offset_ones(span)
    width = 2 * span - 1
    heads = table.shape[0]
    cube = table.reshape(heads, width, width, width)
    section = jnp.einsum("hxyz,cCz->hxycC", cube, ones, precision=exact)
    section = jnp.einsum("hxycC,bBy->hxbcBC", section, ones, precision=exact)
    section = jnp.einsum("hxbcBC,aAx->habcABC", section, ones, precision=exact)
    return section.reshape(heads, span**3, span**3)


def fold_table(pairs, span):
    exact = lax.Precision.HIGHEST
    ones = offset_ones(span)
    heads = pairs.shape[0]
    grid = pairs.reshape(heads, span, span, span, span, span, span)
    section = jnp.einsum("habcABC,aAx->hxbcBC", grid, ones, precision=exact)
    section = jnp.einsum("hxbcBC,bBy->hxycC", section, ones, precision=exact)
    section = jnp.einsum("hxycC,cCz->hxyz", section, ones, precision=exact)
    return section.reshape(heads, -1)


def region_label(start, cells, count):
    places = start + jnp.arange(cells)
    return jnp.where(places < count - WIN, 0, jnp.where(places < count - SHIFT, 1, 2)).astype(
        jnp.int32
    )


def to_windows(array):
    first, second, third = array.shape[:3]
    rest = array.shape[3:]
    shaped = array.reshape((first // WIN, WIN, second // WIN, WIN, third // WIN, WIN) + rest)
    order = (0, 2, 4, 1, 3, 5) + tuple(range(6, 6 + len(rest)))
    return shaped.transpose(order).reshape((-1, WIN**3) + rest)


def from_windows(array, first, second, third):
    feats = array.shape[-1]
    shaped = array.reshape(first // WIN, second // WIN, third // WIN, WIN, WIN, WIN, feats)
    return shaped.transpose(0, 3, 1, 4, 2, 5, 6).reshape(first, second, third, feats)


def forward_depth(pair):
    arrived = shifted(pair[:, :SHIFT], "gx", -1)
    return jnp.concatenate([pair[:, SHIFT:], arrived], 1)


def forward_height(pair):
    arrived = shifted(pair[:, :, :SHIFT], "gy", -1)
    return jnp.concatenate([pair[:, :, SHIFT:], arrived], 2)


def forward_width(pair):
    arrived = shifted(pair[:, :, :, :SHIFT], "gz", -1)
    return jnp.concatenate([pair[:, :, :, SHIFT:], arrived], 3)


def backward_depth(field):
    edge = field.shape[0] - SHIFT
    arrived = shifted(field[edge:], "gx", 1)
    return jnp.concatenate([arrived, field[:edge]], 0)


def backward_height(field):
    edge = field.shape[1] - SHIFT
    arrived = shifted(field[:, edge:], "gy", 1)
    return jnp.concatenate([arrived, field[:, :edge]], 1)


def backward_width(field):
    edge = field.shape[2] - SHIFT
    arrived = shifted(field[:, :, edge:], "gz", 1)
    return jnp.concatenate([arrived, field[:, :, :edge]], 2)


def window_pass(ln_w, dy_w, lab_w, w_qkv, b_qkv, w_proj, bias_full):
    f32 = jnp.float32
    bf16 = jnp.bfloat16
    group, tok, feats = ln_w.shape
    heads = bias_full.shape[0]
    hdim = feats // heads
    scale = hdim ** (-0.5)
    qkv = jnp.einsum("gtc,cf->gtf", ln_w, w_qkv, preferred_element_type=f32) + b_qkv
    qkv = qkv.astype(bf16).reshape(group, tok, 3, heads, hdim)
    query = qkv[:, :, 0].transpose(0, 2, 1, 3)
    keys = qkv[:, :, 1].transpose(0, 2, 1, 3)
    values = qkv[:, :, 2].transpose(0, 2, 1, 3)
    scores = (
        jnp.einsum("ghid,ghjd->ghij", query, keys, preferred_element_type=f32) * scale
        + bias_full[None]
    )
    allowed = (lab_w[:, :, None] == lab_w[:, None, :])[:, None]
    scores = jnp.where(allowed, scores, f32(-1e30))
    top = jnp.max(scores, -1, keepdims=True)
    expo = jnp.exp(scores - top)
    probs = expo / jnp.sum(expo, -1, keepdims=True)
    probs_b = probs.astype(bf16)
    attended = jnp.einsum("ghij,ghjd->ghid", probs_b, values, preferred_element_type=f32)
    attended = attended.transpose(0, 2, 1, 3).reshape(group, tok, feats).astype(bf16)
    grad_att = jnp.einsum("gtc,fc->gtf", dy_w, w_proj, preferred_element_type=f32).astype(bf16)
    proj_part = jnp.einsum("gtf,gtc->fc", attended, dy_w, preferred_element_type=f32)
    grad_heads = grad_att.reshape(group, tok, heads, hdim).transpose(0, 2, 1, 3)
    grad_probs = jnp.einsum("ghid,ghjd->ghij", grad_heads, values, preferred_element_type=f32)
    grad_v = jnp.einsum("ghij,ghid->ghjd", probs_b, grad_heads, preferred_element_type=f32)
    grad_scores = probs * (grad_probs - jnp.sum(probs * grad_probs, -1, keepdims=True))
    rel_part = jnp.sum(grad_scores, 0)
    scores_b = grad_scores.astype(bf16)
    grad_q = jnp.einsum("ghij,ghjd->ghid", scores_b, keys, preferred_element_type=f32) * scale
    grad_k = jnp.einsum("ghij,ghid->ghjd", scores_b, query, preferred_element_type=f32) * scale
    grad_qkv = (
        jnp.stack([grad_q, grad_k, grad_v], 1)
        .transpose(0, 3, 1, 2, 4)
        .reshape(group, tok, 3 * feats)
    )
    bias_part = jnp.sum(grad_qkv, (0, 1))
    qkv_b = grad_qkv.astype(bf16)
    weight_part = jnp.einsum("gtc,gtf->cf", ln_w, qkv_b, preferred_element_type=f32)
    grad_in = jnp.einsum("gtf,cf->gtc", qkv_b, w_qkv, preferred_element_type=f32)
    return (grad_in, (weight_part, bias_part, proj_part, rel_part))


def shards(inputs, d_out, layer_norm_gain, layer_norm_bias, w_qkv, b_qkv, w_proj, rel_bias):
    f32 = jnp.float32
    cells_x, cells_y, cells_z, feats = inputs.shape
    tok = WIN**3
    heads = rel_bias.shape[0]
    xf = inputs.astype(f32)
    centered_input = xf - jnp.mean(xf, -1, keepdims=True)
    inverse_deviation = lax.rsqrt(
        jnp.mean(centered_input * centered_input, -1, keepdims=True) + 1e-05
    )
    normalized_input = centered_input * inverse_deviation
    normalized_tokens = (normalized_input * layer_norm_gain + layer_norm_bias).astype(jnp.bfloat16)
    moved_pair = jnp.stack([normalized_tokens, d_out])
    forward_steps = (forward_depth, forward_height, forward_width)
    backward_steps = (backward_depth, backward_height, backward_width)
    for advance in forward_steps:
        moved_pair = advance(moved_pair)
    label_x = region_label(lax.axis_index("gx") * cells_x, cells_x, cells_x * lax.axis_size("gx"))
    label_y = region_label(lax.axis_index("gy") * cells_y, cells_y, cells_y * lax.axis_size("gy"))
    label_z = region_label(lax.axis_index("gz") * cells_z, cells_z, cells_z * lax.axis_size("gz"))
    labels = label_x[:, None, None] * 9 + label_y[None, :, None] * 3 + label_z[None, None, :]
    bias_full = expand_table(rel_bias, WIN)
    group = cells_y // WIN * (cells_z // WIN)
    win_ln = to_windows(moved_pair[0]).reshape(-1, group, tok, feats)
    win_dy = to_windows(moved_pair[1]).reshape(-1, group, tok, feats)
    win_lab = to_windows(labels).reshape(-1, group, tok)

    def step(carry, item):
        grad_in, parts = window_pass(item[0], item[1], item[2], w_qkv, b_qkv, w_proj, bias_full)
        return (tuple((total + part for total, part in zip(carry, parts))), grad_in)

    start = (
        jnp.zeros((feats, 3 * feats), f32),
        jnp.zeros((3 * feats,), f32),
        jnp.zeros((feats, feats), f32),
        jnp.zeros((heads, tok, tok), f32),
    )
    sums, grad_win = lax.scan(step, start, (win_ln, win_dy, win_lab))
    normalized_output_gradient = from_windows(
        grad_win.reshape(-1, tok, feats), cells_x, cells_y, cells_z
    )
    for retreat in backward_steps:
        normalized_output_gradient = retreat(normalized_output_gradient)
    normalized_gradient = normalized_output_gradient * layer_norm_gain
    input_gradient_norm = inverse_deviation * (
        normalized_gradient
        - jnp.mean(normalized_gradient, -1, keepdims=True)
        - normalized_input * jnp.mean(normalized_gradient * normalized_input, -1, keepdims=True)
    )
    d_x = (d_out.astype(f32) + input_gradient_norm).astype(jnp.bfloat16)
    rel_local = fold_table(sums[3], WIN)
    local_gain = jnp.sum(normalized_output_gradient * normalized_input, (0, 1, 2))
    shift_local = jnp.sum(normalized_output_gradient, (0, 1, 2))
    totals = lax.psum(
        (sums[0], sums[1], sums[2], rel_local, local_gain, shift_local), ("gx", "gy", "gz")
    )
    count = (
        cells_x
        * cells_y
        * cells_z
        * lax.axis_size("gx")
        * lax.axis_size("gy")
        * lax.axis_size("gz")
    )
    inverse_width_factor = float(count) ** (-0.5)
    return (
        d_x,
        totals[0] * inverse_width_factor,
        totals[1] * inverse_width_factor,
        totals[2] * inverse_width_factor,
        totals[3] * inverse_width_factor,
        totals[4] * inverse_width_factor,
        totals[5] * inverse_width_factor,
    )


def solution(mesh):
    placed = (P("gx", "gy", "gz", None), P("gx", "gy", "gz", None), P(), P(), P(), P(), P(), P())
    return jax.shard_map(
        shards,
        mesh=mesh,
        in_specs=placed,
        out_specs=(P("gx", "gy", "gz", None), P(), P(), P(), P(), P(), P()),
        check_vma=False,
    )
```

profile of v0, /device:TPU:0, one launch (start us, length us, event | category | flops | bytes accessed | tf_op | source)
XLA Modules:
  0.0 697.9 jit_solution(15601233751291478034)
XLA Ops:
  7.2 2.4 convert_reduce_fusion
  15.1 5.1 collective-permute-start
  21.9 9.5 %convolution_bitcast_fusion.5 = f32[3,13,7,7,7,7]{1,2,5,3,0,4:T(8,128)S(1)} fusion(f32[3,13,13,7,7]{2,3,1,0,4:T(8,128)S(1)} %convolution_bitcast_fusion.7, s32[7,7]{0,1:T(8,128)S(1)} %subtract_add_fusion), kind=kOutput, calls=%fused_computation.96 | convolution fusion | flops 14608321 | bytes 474124 | tf_op jit(solution)/shard_map/hxycC,bBy->hxbcBC/dot_general | solution.py:30
  32.4 18.0 %collective-permute-start.1 = (bf16[2,28,3,7,96]{4,3,2,1,0:T(8,128)(2,1)S(1)}, bf16[2,28,3,7,96]{4,3,2,1,0:T(8,128)(2,1)S(1)}, u32[]{:S(2)}, u32[]{:S(2)}) collective-permute-start(bf16[2,28,3,7,96]{4,3,2,1,0:T(8,128)(2,1)S(1)} %pad_maximum_fusion.5), channel_id=1, source_target_pairs={{2,0},{4,2},{6,4},{0,6},{3,1},{5,3},{7,5},{1,7},{10,8},{12,10},{14... | collective-permute-start | bytes 677384 | tf_op jit(solution)/shard_map/ppermute | solution.py:13
  51.3 3.9 collective-permute-done.1
  56.1 2.9 copy.74
  60.5 71.1 %convolution_bitcast_fusion.3 = f32[3,7,7,7,7,7,7]{6,4,5,3,2,0,1:T(8,128)} fusion(f32[3,13,7,7,7,7]{1,2,5,3,0,4:T(8,128)S(1)} %convolution_bitcast_fusion.5, pred[7,7,13,1,1,1,1]{2,0,1,6,5,4,3:T(8,128)(4,1)S(1)} %fusion.73), kind=kOutput, calls=%fused_computation.61 | convolution fusion | flops 55059736 | bytes 1786981 | tf_op jit(solution)/shard_map/hxbcBC,aAx->habcABC/dot_general | solution.py:31
  131.7 59.5 %copy.82 = f32[3,7,7,7,7,7,7]{3,2,1,6,5,4,0:T(8,128)} copy(f32[3,7,7,7,7,7,7]{6,4,5,3,2,0,1:T(8,128)} %convolution_bitcast_fusion.3) | data formatting | bytes 2823576
  191.2 20.9 %add.240 = f32[3,343,343]{1,2,0:T(8,128)} reshape(f32[3,7,7,7,7,7,7]{3,2,1,6,5,4,0:T(8,128)} %copy.82) | data formatting | bytes 2823576 | tf_op jit(solution)/shard_map/while/body/eval_jaxpr/add | solution.py:113
  213.2 2.6 fusion.67
  217.5 2.1 pad_maximum_fusion.2
  221.5 2.5 copy.81
  225.9 2.5 copy.83
  228.5 134.0 %while.20 = (s32[]{:T(128)}, f32[96,288]{1,0:T(8,128)}, f32[288]{0:T(512)S(1)}, f32[96,96]{1,0:T(8,128)S(1)}, f32[3,343,343]{1,2,0:T(8,128)}, /*index=5*/f32[4,4...) while((s32[]{:T(128)}, f32[96,288]{1,0:T(8,128)}, ...), condition=%wide.wide.region_8.9_spmd.clone, body=%wide.wide.region_2.8_spmd.clone.sunk | while | flops 848489408 | bytes 107633568 | solution.py:183
  231.1 7.0 fusion.174
  238.3 6.9 multiply_reduce_fusion.4
  245.2 4.2 fusion.176
  253.8 2.1 fusion.180
  257.2 3.6 fusion.182
  263.4 7.0 fusion.174
  270.7 6.9 multiply_reduce_fusion.4
  277.6 4.2 fusion.176
  286.2 2.1 fusion.180
  288.3 2.7 select_add_fusion.7
  291.0 3.6 fusion.182
  297.2 7.0 fusion.174
  304.5 6.9 multiply_reduce_fusion.4
  311.4 4.2 fusion.176
  320.0 2.1 fusion.180
  322.1 2.7 select_add_fusion.7
  324.8 3.6 fusion.182
  331.0 7.0 fusion.174
  338.3 6.9 multiply_reduce_fusion.4
  345.2 4.2 fusion.176
  353.8 2.1 fusion.180
  355.9 2.7 select_add_fusion.7
  358.6 3.6 fusion.182
  362.5 3.4 copy.84
  368.9 20.0 %reshape.160 = f32[3,7,7,7,7,7,7]{3,2,1,6,5,4,0:T(8,128)} reshape(f32[3,343,343]{1,2,0:T(8,128)S(1)} %copy-done) | data formatting | bytes 2823576 | tf_op jit(solution)/shard_map/reshape | solution.py:39
  388.9 59.6 %copy.88 = f32[3,7,7,7,7,7,7]{1,6,4,5,3,2,0:T(8,128)} copy(f32[3,7,7,7,7,7,7]{3,2,1,6,5,4,0:T(8,128)} %reshape.160) | data formatting | bytes 2823576 | tf_op jit(solution)/shard_map/reshape | solution.py:39
  450.1 25.1 %convolution_bitcast_fusion.4 = f32[3,13,7,7,7,7]{1,5,4,3,2,0:T(8,128)} fusion(f32[3,7,7,7,7,7,7]{1,6,4,5,3,2,0:T(8,128)} %copy.88, s32[7,7]{0,1:T(8,128)S(1)} %copy-done.22), kind=kOutput, calls=%fused_computation.95 | convolution fusion | flops 55060372 | bytes 1786540 | tf_op jit(solution)/shard_map/habcABC,aAx->hxbcBC/dot_general | solution.py:40
  475.2 12.8 %copy.89 = f32[3,13,7,7,7,7]{2,3,4,5,1,0:T(8,128)} copy(f32[3,13,7,7,7,7]{1,5,4,3,2,0:T(8,128)} %convolution_bitcast_fusion.4) | data formatting | bytes 749112 | tf_op jit(solution)/shard_map/habcABC,aAx->hxbcBC/transpose | solution.py:40
  493.0 5.4 convolution_bitcast_fusion.6
  499.7 121.2 %all-reduce.3.cloned.1.call-done = f32[96,288]{1,0:T(8,128)} async-done(((f32[96,288]{1,0:T(8,128)}), f32[96,288]{1,0:T(8,128)}) %all-reduce.3.cloned.1.call-update) | async-done | bytes 110608 | tf_op jit(solution)/shard_map/psum | solution.py:199
  622.5 3.9 slice_reduce_fusion
  628.2 5.9 fusion.61
  634.2 43.7 %all-reduce = (f32[288]{0:T(512)S(1)}, f32[96,96]{1,0:T(8,128)S(1)}, f32[3,2197]{1,0:T(4,128)S(1)}, f32[96]{0:T(128)S(1)}, f32[96]{0:T(128)S(1)}) all-reduce(f32[288]{0:T(512)S(1)} %get-tuple-element.80, f32[96,96]{1,0:T(8,128)S(1)} %get-tuple-element.81, ...), channel_id=1, replica_groups=mesh['gx'=4,'gy'=4,'gz'=2] {'gx','gy','gz'}, use_global_device_ids=true, to_apply=%region_12.13 | all-reduce | flops 16287 | bytes 130296 | tf_op jit(solution)/shard_map/psum | solution.py:199
  682.9 8.0 %fusion.60 = bf16[28,28,7,96]{3,2,1,0:T(8,128)(2,1)} fusion(bf16[28,28,7,96]{3,2,1,0:T(8,128)(2,1)S(1)} %copy-done.2, bf16[28,28,7,96]{3,2,1,0:T(8,128)(2,1)S(1)} %copy-done.6, f32[28,28,7]{2,1,0:T(8,128)S(1)} %broadcast_multiply_fusion, f32[28,28,7]{2,1,0:T(8,128)S(1)} %broadcast_multiply_fusion.1, f32[96]{0:T(128)S(1)} %copy-done.26, ...), kind=kLoop, calls=%fused_computation.78 | loop fusion | flops 6322176 | bytes 5356672 | tf_op jit(solution)/shard_map/convert_element_type | solution.py:195
  (214 shorter events, 66.8 us)
Async XLA Ops:
  7.2 4.6 copy-start.25
  7.2 4.6 copy-start.27
  7.2 613.7 %all-reduce.3.cloned.1.call-start = ((), (), s32[]{:S(2)}) async-start(), calls=%async_computation | async-start | bytes 294912 | tf_op jit(solution)/shard_map/psum | solution.py:199
  9.8 4.1 copy-start.16
  9.8 5.2 copy-start.5
  13.8 6.4 copy-start.24
  15.1 17.2 %collective-permute-start = (bf16[2,3,28,7,96]{4,3,2,1,0:T(8,128)(2,1)S(1)}, bf16[2,3,28,7,96]{4,3,2,1,0:T(8,128)(2,1)S(1)}, u32[]{:S(2)}, u32[]{:S(2)}) collective-permute-start(bf16[2,3,28,7,96]{4,3,2,1,0:T(8,128)(2,1)S(1)} %pad_maximum_fusion.6), channel_id=1, source_target_pairs={{8,0},{16,8},{24,16},{0,24},{9,1},{17,9},{25,17},{1,25},{10,2},{18... | collective-permute-start | bytes 677384 | tf_op jit(solution)/shard_map/ppermute | solution.py:13
  20.2 30.2 %copy-start.21 = (s32[7,7]{0,1:T(8,128)}, s32[7,7]{0,1:T(8,128)S(1)}, u32[]{:S(2)}) copy-start(s32[7,7]{0,1:T(8,128)S(1)} %subtract_add_fusion) | copy-start | bytes 592
  20.5 11.0 %copy-start.12 = (bf16[1,28,28,7,96]{4,3,2,1,0:T(8,128)(2,1)S(1)}, bf16[1,28,28,7,96]{4,3,2,1,0:T(8,128)(2,1)}, u32[]{:S(2)}) copy-start(bf16[1,28,28,7,96]{4,3,2,1,0:T(8,128)(2,1)} %copy-done.11) | copy-start | bytes 3161092
  32.4 22.8 %collective-permute-start.1 = (bf16[2,28,3,7,96]{4,3,2,1,0:T(8,128)(2,1)S(1)}, bf16[2,28,3,7,96]{4,3,2,1,0:T(8,128)(2,1)S(1)}, u32[]{:S(2)}, u32[]{:S(2)}) collective-permute-start(bf16[2,28,3,7,96]{4,3,2,1,0:T(8,128)(2,1)S(1)} %pad_maximum_fusion.5), channel_id=1, source_target_pairs={{2,0},{4,2},{6,4},{0,6},{3,1},{5,3},{7,5},{1,7},{10,8},{12,10},{14... | collective-permute-start | bytes 677384 | tf_op jit(solution)/shard_map/ppermute | solution.py:13
  55.2 3.7 copy-start.19
  59.0 156.9 %collective-permute-start.2 = (bf16[2,28,28,3,96]{4,0,3,2,1:T(2,128)(2,1)}, bf16[2,28,28,3,96]{4,0,3,2,1:T(2,128)(2,1)}, u32[]{:S(2)}, u32[]{:S(2)}) collective-permute-start(bf16[2,28,28,3,96]{4,0,3,2,1:T(2,128)(2,1)} %copy.74), channel_id=1, source_target_pairs={{1,0},{0,1},{3,2},{2,3},{5,4},{4,5},{7,6},{6,7},{9,8},{8,9},{11,10... | collective-permute-start | bytes 2709512 | tf_op jit(solution)/shard_map/ppermute | solution.py:13
  224.0 4.5 copy-start.17
  224.0 4.5 copy-start.20
  224.1 4.4 copy-start.23
  228.7 9.3 %copy-start.9 = (bf16[4,4,343,96]{2,3,1,0:T(8,128)(2,1)}, bf16[4,4,343,96]{2,3,1,0:T(8,128)(2,1)S(1)}, u32[]{:S(2)}) copy-start(bf16[4,4,343,96]{2,3,1,0:T(8,128)(2,1)S(1)} %get-tuple-element.416) | copy-start | bytes 3161092 | tf_op jit(solution)/shard_map/while
  228.7 9.3 %copy-start.13 = (bf16[4,4,343,96]{2,3,1,0:T(8,128)(2,1)}, bf16[4,4,343,96]{2,3,1,0:T(8,128)(2,1)S(1)}, u32[]{:S(2)}) copy-start(bf16[4,4,343,96]{2,3,1,0:T(8,128)(2,1)S(1)} %get-tuple-element.421) | copy-start | bytes 3161092 | tf_op jit(solution)/shard_map/while
  238.3 6.9 slice-start
  238.3 6.9 slice-start.1
  257.2 3.6 copy-start.14
  257.2 3.8 copy-start.10
  261.1 9.3 %copy-start.9 = (bf16[4,4,343,96]{2,3,1,0:T(8,128)(2,1)}, bf16[4,4,343,96]{2,3,1,0:T(8,128)(2,1)S(1)}, u32[]{:S(2)}) copy-start(bf16[4,4,343,96]{2,3,1,0:T(8,128)(2,1)S(1)} %get-tuple-element.416) | copy-start | bytes 3161092 | tf_op jit(solution)/shard_map/while
  261.1 9.3 %copy-start.13 = (bf16[4,4,343,96]{2,3,1,0:T(8,128)(2,1)}, bf16[4,4,343,96]{2,3,1,0:T(8,128)(2,1)S(1)}, u32[]{:S(2)}) copy-start(bf16[4,4,343,96]{2,3,1,0:T(8,128)(2,1)S(1)} %get-tuple-element.421) | copy-start | bytes 3161092 | tf_op jit(solution)/shard_map/while
  270.7 6.9 slice-start
  270.7 6.9 slice-start.1
  291.0 3.8 copy-start.10
  294.9 9.3 %copy-start.9 = (bf16[4,4,343,96]{2,3,1,0:T(8,128)(2,1)}, bf16[4,4,343,96]{2,3,1,0:T(8,128)(2,1)S(1)}, u32[]{:S(2)}) copy-start(bf16[4,4,343,96]{2,3,1,0:T(8,128)(2,1)S(1)} %get-tuple-element.416) | copy-start | bytes 3161092 | tf_op jit(solution)/shard_map/while
  294.9 9.3 %copy-start.13 = (bf16[4,4,343,96]{2,3,1,0:T(8,128)(2,1)}, bf16[4,4,343,96]{2,3,1,0:T(8,128)(2,1)S(1)}, u32[]{:S(2)}) copy-start(bf16[4,4,343,96]{2,3,1,0:T(8,128)(2,1)S(1)} %get-tuple-element.421) | copy-start | bytes 3161092 | tf_op jit(solution)/shard_map/while
  304.4 6.9 slice-start
  304.4 6.9 slice-start.1
  324.8 3.6 copy-start.14
  324.8 3.8 copy-start.10
  328.7 9.3 %copy-start.9 = (bf16[4,4,343,96]{2,3,1,0:T(8,128)(2,1)}, bf16[4,4,343,96]{2,3,1,0:T(8,128)(2,1)S(1)}, u32[]{:S(2)}) copy-start(bf16[4,4,343,96]{2,3,1,0:T(8,128)(2,1)S(1)} %get-tuple-element.416) | copy-start | bytes 3161092 | tf_op jit(solution)/shard_map/while
  328.7 9.3 %copy-start.13 = (bf16[4,4,343,96]{2,3,1,0:T(8,128)(2,1)}, bf16[4,4,343,96]{2,3,1,0:T(8,128)(2,1)S(1)}, u32[]{:S(2)}) copy-start(bf16[4,4,343,96]{2,3,1,0:T(8,128)(2,1)S(1)} %get-tuple-element.421) | copy-start | bytes 3161092 | tf_op jit(solution)/shard_map/while
  338.3 6.9 slice-start
  338.3 6.9 slice-start.1
  358.6 3.6 copy-start.14
  358.6 3.8 copy-start.10
  367.1 81.4 %collective-permute-start.3 = (f32[3,28,7,96]{3,2,1,0:T(8,128)}, f32[3,28,7,96]{3,2,1,0:T(8,128)S(1)}, u32[]{:S(2)}, u32[]{:S(2)}) collective-permute-start(f32[3,28,7,96]{3,2,1,0:T(8,128)} %slice.79), channel_id=1, source_target_pairs={{24,0},{0,8},{8,16},{16,24},{25,1},{1,9},{9,17},{17,25},{26,2},{2,... | collective-permute-start | bytes 677384 | tf_op jit(solution)/shard_map/ppermute | solution.py:13
  388.9 59.6 %copy-start.4 = (f32[25,28,7,96]{3,2,1,0:T(8,128)S(1)}, f32[25,28,7,96]{3,2,1,0:T(8,128)}, u32[]{:S(2)}) copy-start(f32[25,28,7,96]{3,2,1,0:T(8,128)} %slice.80) | copy-start | bytes 5644804
  449.3 38.7 %collective-permute-start.4 = (f32[28,3,7,96]{3,2,1,0:T(8,128)}, f32[28,3,7,96]{3,2,1,0:T(8,128)}, u32[]{:S(2)}, u32[]{:S(2)}) collective-permute-start(f32[28,3,7,96]{3,2,1,0:T(8,128)} %pad_maximum_fusion.4), channel_id=1, source_target_pairs={{6,0},{0,2},{2,4},{4,6},{7,1},{1,3},{3,5},{5,7},{14,8},{8,10},{10,... | collective-permute-start | bytes 677384 | tf_op jit(solution)/shard_map/ppermute | solution.py:13
  488.0 5.0 copy-start.3
  489.6 8.8 %copy-start.15 = (f32[28,28,7,96]{3,2,1,0:T(8,128)}, f32[28,28,7,96]{3,2,1,0:T(8,128)S(1)}, u32[]{:S(2)}) copy-start(f32[28,28,7,96]{3,2,1,0:T(8,128)S(1)} %fusion.63) | copy-start | bytes 6322180
  491.3 135.1 %collective-permute-start.5 = (f32[28,28,3,96]{3,1,2,0:T(8,128)}, f32[28,28,3,96]{3,1,2,0:T(8,128)S(1)}, u32[]{:S(2)}, u32[]{:S(2)}) collective-permute-start(f32[28,28,3,96]{3,1,2,0:T(8,128)} %copy.86), channel_id=1, source_target_pairs={{1,0},{0,1},{3,2},{2,3},{5,4},{4,5},{7,6},{6,7},{9,8},{8,9},{11,10... | collective-permute-start | bytes 2709512 | tf_op jit(solution)/shard_map/ppermute | solution.py:13
  622.5 5.3 copy-start.2
  622.5 5.3 copy-start.26
  627.8 6.4 copy-start.8
  628.2 54.6 %copy-start.6 = (bf16[28,28,7,96]{3,2,1,0:T(8,128)(2,1)S(1)}, bf16[28,28,7,96]{3,2,1,0:T(8,128)(2,1)}, u32[]{:S(2)}) copy-start(bf16[28,28,7,96]{3,2,1,0:T(8,128)(2,1)} %param.11) | copy-start | bytes 3161092
  (7 other events, 16.2 us)
Sparse Core Ops, SparseCore 0:
  498.6 122.2 all-reduce.2
where the time goes:
time: 706 us; the launch traced here: 698 us
  matrix products  211 us (30%)
  local copies, waits for them, and re-layouts  203 us (29%)
  waiting for transfers between devices  125 us (18%)
  other arithmetic  73.7 us (10%)
  blocking collectives  43.7 us (6%)
  starting transfers between devices  26.1 us (4%)
  between operations  14.7 us (2%)
    psum x1, waiting for transfers between devices, shards(): lax.psum((sums[0], sums[1], sums[2], rel_local, local_gain, shift_local),...  121 us
    reshape x2, local copies, waits for them, and re-layouts, fold_table(): grid = pairs.reshape(heads, span, span, span, span, span, span)  79.7 us
    dot_general x1, matrix products, expand_table(): section = jnp.einsum('hxbcBC,aAx->habcABC', section, ones, precision=exact)  71.1 us
    unnamed x51, local copies, waits for them, and re-layouts  67.5 us
    psum x1, blocking collectives, shards(): lax.psum((sums[0], sums[1], sums[2], rel_local, local_gain, shift_local),...  43.7 us
    sub x4, matrix products, window_pass(): expo = jnp.exp(scores - top)  27.8 us
    dot_general x4, matrix products, window_pass(): jnp.einsum('ghid,ghjd->ghij', grad_heads, values, preferred_element_type=...  27.7 us
    ppermute x6, starting transfers between devices, shifted(): return lax.ppermute(block, axis, route)  26 us
  transfers between devices with their start and end apart: 7, of which 2 were waited for; matrix products, arithmetic and copies ran while one was open for 43% of the time, Pallas kernels for 0%

commit v1 on v0

v1 whole, which is shorter than its diff:
```python
import functools

import jax
import jax.numpy as jnp
from jax import lax
from jax.experimental import pallas as pl
from jax.experimental.pallas import tpu as pltpu
from jax.sharding import PartitionSpec as P

WIN = 7
SHIFT = 3
TOK = WIN**3
ROWS = 344
LANES = 384
SLAB = 8 * WIN * WIN
SPAN = 2 * WIN - 1
WIDE = 1152
TABLE = 2304
HID = 112
AUG = 80
BIG = 1e30
F32 = jnp.float32
BF16 = jnp.bfloat16
NN = (((1,), (0,)), ((), ()))
NT = (((1,), (1,)), ((), ()))


def dot(left, right, dims=NN):
    return lax.dot_general(left, right, dims, preferred_element_type=F32)


def halves(value):
    high = value.astype(BF16)
    return high, (value - high.astype(F32)).astype(BF16)


def thirds(value):
    high = value.astype(BF16)
    rest = value - high.astype(F32)
    mid = rest.astype(BF16)
    return high, mid, (rest - mid.astype(F32)).astype(BF16)


def seventh(count):
    return (count * 9363) >> 16


def places(token):
    upper = seventh(token)
    first = seventh(upper)
    return first, upper - WIN * first, token - WIN * upper


def spread_ones():
    token = lax.broadcasted_iota(jnp.int32, (1, LANES), 1)
    first, second, third = places(token)
    target = jnp.where(token < TOK, first * SPAN * SPAN + second * SPAN + third, -1)
    row = lax.broadcasted_iota(jnp.int32, (WIDE, LANES), 0)
    return jnp.where(row == target, 1.0, 0.0).astype(BF16)


def shear(rows, sign):
    steps = WIN - 1 - lax.broadcasted_iota(jnp.int32, rows.shape, 0)
    for bit in (1, 2, 4):
        moved = pltpu.roll(rows, bit if sign > 0 else TABLE - bit, 1)
        rows = jnp.where((steps & bit) != 0, moved, rows)
    return rows


def offset_of(first, second):
    return (WIN - 1 - first) * SPAN * SPAN + (WIN - 1 - second) * SPAN


def expand_body(table_ref, bias_ref, base_ref, ones_ref, wide_ref):
    ones_ref[...] = spread_ones()
    heads = bias_ref.shape[0]
    for head in range(heads):
        row = jnp.broadcast_to(table_ref[head : head + 1, :], (8, TABLE))
        base_ref[...] = shear(row, -1)
        for first in range(WIN):
            for second in range(WIN):
                at = offset_of(first, second)
                rows = 8 * (first * WIN + second)
                wide_ref[rows : rows + 8, :] = base_ref[:, at : at + WIDE]
        high, mid, low = thirds(wide_ref[...])
        full = (dot(high, ones_ref[...]) + dot(mid, ones_ref[...])) + dot(low, ones_ref[...])
        for group in range(WIN * WIN):
            bias_ref[head, WIN * group : WIN * group + WIN, :] = full[8 * group : 8 * group + WIN]
        bias_ref[head, TOK:ROWS, :] = jnp.zeros((ROWS - TOK, LANES), F32)


def expand_table(table, heads, interpret=False):
    return pl.pallas_call(
        expand_body,
        out_shape=jax.ShapeDtypeStruct((heads, ROWS, LANES), F32),
        scratch_shapes=[
            pltpu.VMEM((8, TABLE), F32),
            pltpu.VMEM((WIDE, LANES), BF16),
            pltpu.VMEM((SLAB, WIDE), F32),
        ],
        cost_estimate=pl.CostEstimate(flops=9_000_000_000, bytes_accessed=2_000_000, transcendentals=0),
        interpret=interpret,
        name="expand",
    )(table)


def fold_body(pairs_ref, table_ref, rows_ref, ones_ref, total_ref):
    ones_ref[...] = spread_ones()
    heads = pairs_ref.shape[0]
    table_ref[...] = jnp.zeros(table_ref.shape, F32)
    rows_ref[...] = jnp.zeros(rows_ref.shape, F32)
    for head in range(heads):
        for group in range(WIN * WIN):
            rows_ref[8 * group : 8 * group + WIN, :] = pairs_ref[head, WIN * group : WIN * group + WIN, :]
        high, low = halves(rows_ref[...])
        wide = dot(high, ones_ref[...], NT) + dot(low, ones_ref[...], NT)
        total_ref[...] = jnp.zeros(total_ref.shape, F32)
        for first in range(WIN):
            for second in range(WIN):
                at = offset_of(first, second)
                rows = 8 * (first * WIN + second)
                total_ref[:, at : at + WIDE] = total_ref[:, at : at + WIDE] + wide[rows : rows + 8]
        sheared = shear(total_ref[...], 1)
        table_ref[head : head + 1, :] = jnp.sum(sheared, 0, keepdims=True)


def fold_table(pairs, interpret=False):
    return pl.pallas_call(
        fold_body,
        out_shape=jax.ShapeDtypeStruct((8, TABLE), F32),
        scratch_shapes=[
            pltpu.VMEM((SLAB, LANES), F32),
            pltpu.VMEM((WIDE, LANES), BF16),
            pltpu.VMEM((8, TABLE), F32),
        ],
        interpret=interpret,
        name="fold",
    )(pairs)


def window_body(
    flag_ref, xd_ref, bias_ref, gain_ref, shift_ref, wside_ref, wtrans_ref, wproj_ref, wq_ref, wkv_ref,
    dx_ref, pair_ref, gq_ref, gkv_ref, gproj_ref, vec_ref,
    pack_ref, unpack_ref, kmask_ref, qmask_ref, score_ref, expo_ref, grad_ref, qdiag_ref, odiag_ref,
    kaug_ref, vaug_ref, attn_ref, dq_ref,
):
    heads = pair_ref.shape[0]
    feats = wproj_ref.shape[0]
    hdim = feats // heads
    scale = hdim ** (-0.5)
    at = [pl.program_id(axis) for axis in range(3)]
    first_step = (at[0] == 0) & (at[1] == 0) & (at[2] == 0)

    @pl.when(first_step)
    def _():
        place = lax.broadcasted_iota(jnp.int32, (LANES, SLAB), 1)
        token = lax.broadcasted_iota(jnp.int32, (LANES, SLAB), 0)
        target = jnp.where((place & 7) == 7, -1, place - (place >> 3))
        pack_ref[...] = jnp.where(token == target, 1.0, 0.0).astype(BF16)
        place = lax.broadcasted_iota(jnp.int32, (SLAB, LANES), 0)
        token = lax.broadcasted_iota(jnp.int32, (SLAB, LANES), 1)
        target = jnp.where((place & 7) == 7, -1, place - (place >> 3))
        unpack_ref[...] = jnp.where(token == target, 1.0, 0.0).astype(BF16)
        row = lax.broadcasted_iota(jnp.int32, (ROWS, 128), 0)
        lane = lax.broadcasted_iota(jnp.int32, (ROWS, 128), 1)
        late = [(part >= WIN - SHIFT).astype(F32) for part in places(row)]
        value = jnp.zeros((ROWS, 128), F32)
        for axis in range(3):
            value = jnp.where(lane == 64 + 2 * axis, -BIG * (1.0 - late[axis]), value)
            value = jnp.where(lane == 65 + 2 * axis, -BIG * late[axis], value)
        value = jnp.where((lane == 70) & (row >= TOK), -BIG, value)
        kmask_ref[...] = value
        row = lax.broadcasted_iota(jnp.int32, (16, LANES), 0)
        lane = lax.broadcasted_iota(jnp.int32, (16, LANES), 1)
        late = [(part >= WIN - SHIFT).astype(F32) for part in places(lane)]
        value = jnp.where(row == 6, 1.0, 0.0)
        for axis in range(3):
            value = jnp.where(row == 2 * axis, late[axis], value)
            value = jnp.where(row == 2 * axis + 1, 1.0 - late[axis], value)
        qmask_ref[...] = value.astype(BF16)
        for ref in (pair_ref, gq_ref, gkv_ref, gproj_ref, vec_ref, qdiag_ref, odiag_ref):
            ref[...] = jnp.zeros(ref.shape, ref.dtype)

    block = xd_ref[...].astype(F32).reshape(SLAB, 256).astype(BF16)
    packed = dot(pack_ref[...], block)
    dy_tok = packed[:, 128:].astype(BF16)
    x_t = packed[:, :128].T[:feats]
    dy_t = packed[:, 128:].T[:feats]
    mu = jnp.sum(x_t, 0, keepdims=True) * (1.0 / feats)
    centered = x_t - mu
    rstd = lax.rsqrt(jnp.sum(centered * centered, 0, keepdims=True) * (1.0 / feats) + 1e-05)
    xhat = centered * rstd
    valid = (lax.broadcasted_iota(jnp.int32, (1, LANES), 1) < TOK).astype(F32)
    normed = (xhat * gain_ref[...] + shift_ref[...]) * valid
    row = lax.broadcasted_iota(jnp.int32, (128 - feats, LANES), 0)
    tail = jnp.where(row < 3, valid, 0.0)
    norm_full = jnp.concatenate([normed, tail], 0)
    norm_t = norm_full[:HID].astype(BF16)
    norm_tok = norm_full.T[:ROWS].astype(BF16)

    lane = lax.broadcasted_iota(jnp.int32, (1, 128), 1)
    flags = jnp.where(lane == 70, 1.0, 0.0)
    for axis in range(3):
        last = (at[axis] == pl.num_programs(axis) - 1).astype(F32) * flag_ref[axis]
        flags = jnp.where((lane == 64 + 2 * axis) | (lane == 65 + 2 * axis), last, flags)
    kmask = kmask_ref[...] * flags
    ones = jnp.where((lane >= 64) & (lane < 67), 1.0, 0.0)
    side = dot(norm_tok, wside_ref[...])
    for head in range(heads):
        kaug_ref[head] = (side[:, 128 * head : 128 * head + 128] + kmask).astype(BF16)
        base = 128 * (heads + head)
        vaug_ref[head] = (side[:, base : base + 128] + ones).astype(BF16)
    turned = dot(wtrans_ref[...], norm_t)
    q_at = 48 * heads
    k_at = q_at + feats
    q_t = turned[q_at : q_at + feats].astype(BF16)
    k_t = turned[k_at : k_at + feats].astype(BF16)
    do_t = dot(wproj_ref[...], dy_tok[:, :feats], NT).astype(BF16).astype(F32)
    scaled = q_t.astype(F32) * (scale * 1.4426950408889634)

    for head in range(heads):
        lo, hi = hdim * head, hdim * (head + 1)
        span = slice(LANES * head, LANES * (head + 1))
        q_high, q_low = halves(scaled[lo:hi])
        q_aug = jnp.concatenate([q_high, q_low, qmask_ref[...]], 0)
        score = dot(kaug_ref[head, :, :AUG], q_aug) + bias_ref[head]
        score_ref[...] = score
        top = jnp.max(score, 0, keepdims=True)
        expo = jnp.exp2(score_ref[...] - top).astype(BF16)
        expo_ref[:, span] = expo
        v_t = turned[48 * head : 48 * head + 48].astype(BF16)
        out = dot(v_t[:, :ROWS], expo_ref[:, span])
        inverse = 1.0 / out[hdim : hdim + 1]
        out = out[:hdim] * inverse
        attn_ref[lo:hi, :] = out.astype(BF16)
        grad_out = do_t[lo:hi]
        mean = jnp.sum(out * grad_out, 0, keepdims=True) * (-inverse)
        o_high, o_low = halves(grad_out * inverse)
        m_high, m_mid, m_low = thirds(mean)
        row16 = lax.broadcasted_iota(jnp.int32, (16, LANES), 0)
        m_rows = jnp.where(
            row16 == 0,
            m_high.astype(F32),
            jnp.where(row16 == 1, m_mid.astype(F32), jnp.where(row16 == 2, m_low.astype(F32), 0.0)),
        ).astype(BF16)
        o_aug = jnp.concatenate([o_high, o_low, m_rows], 0)
        grads = dot(vaug_ref[head, :, :AUG], o_aug) * expo_ref[:, span].astype(F32)
        pair_ref[head] = pair_ref[head] + grads
        grad_ref[:, span] = grads.astype(BF16)
        qdiag_ref[lo:hi, span] = q_t[lo:hi]
        odiag_ref[lo:hi, span] = o_high
        dq_ref[lo:hi, :] = (dot(k_t[lo:hi, :ROWS], grad_ref[:, span]) * scale).astype(BF16)

    dk = (dot(grad_ref[...], qdiag_ref[...], NT) * scale).astype(BF16)
    dv = dot(expo_ref[...], odiag_ref[...], NT).astype(BF16)
    dkv = jnp.concatenate([dk, dv], 1)
    dq = dq_ref[...]
    gq_ref[...] = gq_ref[...] + dot(norm_t, dq, NT)
    gkv_ref[...] = gkv_ref[...] + dot(norm_t[:, :ROWS], dkv)
    gproj_ref[...] = gproj_ref[...] + dot(attn_ref[...], dy_tok[:, :feats])
    dkv_all = jnp.concatenate([dkv, jnp.zeros((LANES - ROWS, 2 * feats), BF16)], 0)
    grad_in = dot(wq_ref[...], dq) + dot(wkv_ref[...], dkv_all, NT)
    vec_ref[0] = vec_ref[0] + grad_in * xhat
    vec_ref[1] = vec_ref[1] + grad_in
    dhat = grad_in * gain_ref[...]
    mean_one = jnp.sum(dhat, 0, keepdims=True) * (1.0 / feats)
    mean_two = jnp.sum(dhat * xhat, 0, keepdims=True) * (1.0 / feats)
    d_x = (dy_t + rstd * (dhat - mean_one - xhat * mean_two)).astype(BF16)
    spread = dot(unpack_ref[...], d_x, NT)
    dx_ref[...] = spread.reshape(WIN, WIN, 8, feats).astype(BF16)


def window_call(flags, xd, bias, gain, shift, wside, wtrans, wproj, wq, wkv, heads, interpret=False):
    feats = wproj.shape[0]
    grid = (xd.shape[0] // WIN, xd.shape[1] // WIN, xd.shape[2] // 8)

    def whole(array):
        zeros = (0,) * array.ndim
        return pl.BlockSpec(array.shape, lambda *_: zeros)

    def total(shape):
        zeros = (0,) * len(shape)
        return pl.BlockSpec(shape, lambda *_: zeros), jax.ShapeDtypeStruct(shape, F32)

    def tile(width):
        return pl.BlockSpec((WIN, WIN, 8, width), lambda i, j, k: (i, j, k, 0))

    sums = [
        total((heads, ROWS, LANES)),
        total((HID, feats)),
        total((HID, 2 * feats)),
        total((feats, feats)),
        total((2, feats, LANES)),
    ]
    return pl.pallas_call(
        window_body,
        grid=grid,
        in_specs=[pl.BlockSpec(memory_space=pltpu.SMEM), tile(256)]
        + [whole(a) for a in (bias, gain, shift, wside, wtrans, wproj, wq, wkv)],
        out_specs=[tile(feats)] + [s[0] for s in sums],
        out_shape=[jax.ShapeDtypeStruct(xd.shape[:3] + (feats,), BF16)] + [s[1] for s in sums],
        scratch_shapes=[
            pltpu.VMEM((LANES, SLAB), BF16),
            pltpu.VMEM((SLAB, LANES), BF16),
            pltpu.VMEM((ROWS, 128), F32),
            pltpu.VMEM((16, LANES), BF16),
            pltpu.VMEM((ROWS, LANES), F32),
            pltpu.VMEM((ROWS, heads * LANES), BF16),
            pltpu.VMEM((ROWS, heads * LANES), BF16),
            pltpu.VMEM((feats, heads * LANES), BF16),
            pltpu.VMEM((feats, heads * LANES), BF16),
            pltpu.VMEM((heads, ROWS, 128), BF16),
            pltpu.VMEM((heads, ROWS, 128), BF16),
            pltpu.VMEM((feats, LANES), BF16),
            pltpu.VMEM((feats, LANES), BF16),
        ],
        compiler_params=pltpu.CompilerParams(
            dimension_semantics=("arbitrary",) * 3, vmem_limit_bytes=60 * 1024 * 1024
        ),
        interpret=interpret,
        name="windows",
    )(flags, xd, bias, gain, shift, wside, wtrans, wproj, wq, wkv)


def side_weights(w_qkv, b_qkv, heads):
    feats = w_qkv.shape[0]
    hdim = feats // heads
    parts = thirds(b_qkv)
    full = jnp.concatenate(
        [w_qkv] + [p[None] for p in parts] + [jnp.zeros((128 - feats - 3, 3 * feats), BF16)], 0
    )
    cols = full.reshape(128, 3, heads, hdim)
    pad = jnp.zeros((128, 2, heads, 128 - 2 * hdim), BF16)
    wside = jnp.concatenate([cols[:, 1:], cols[:, 1:], pad], -1).reshape(128, 2 * heads * 128)
    v_rows = cols[:HID, 2].transpose(1, 2, 0)
    one = (jnp.arange(HID)[None, None, :] == feats) & (jnp.arange(16)[None, :, None] == 0)
    one = jnp.broadcast_to(one.astype(BF16), (heads, 16, HID))
    v_rows = jnp.concatenate([v_rows, one], 1).reshape(48 * heads, HID)
    qk_rows = full[:HID, : 2 * feats].T
    return wside, jnp.concatenate([v_rows, qk_rows], 0)


def shifted(block, axis, distance):
    devices = range(lax.axis_size(axis))
    route = [((i - distance) % len(devices), i) for i in devices]
    return lax.ppermute(block, axis, route)


def forward(field, dim, axis):
    arrived = shifted(lax.slice_in_dim(field, 0, SHIFT, axis=dim), axis, -1)
    return jnp.concatenate([lax.slice_in_dim(field, SHIFT, None, axis=dim), arrived], dim)


def backward(field, dim, axis):
    edge = field.shape[dim] - SHIFT
    arrived = shifted(lax.slice_in_dim(field, edge, None, axis=dim), axis, 1)
    return jnp.concatenate([arrived, lax.slice_in_dim(field, 0, edge, axis=dim)], dim)


def shards(inputs, d_out, layer_norm_gain, layer_norm_bias, w_qkv, b_qkv, w_proj, rel_bias):
    cells_x, cells_y, cells_z, feats = inputs.shape
    heads = rel_bias.shape[0]
    pad = jnp.zeros(inputs.shape[:3] + (128 - feats,), BF16)
    xd = jnp.concatenate([inputs, pad, d_out, pad], -1)
    for dim, axis in enumerate(("gx", "gy", "gz")):
        xd = forward(xd, dim, axis)
    deep = cells_z // WIN
    xd = xd.reshape(cells_x, cells_y, deep, WIN, 256)
    xd = jnp.pad(xd, ((0, 0), (0, 0), (0, 0), (0, 1), (0, 0))).reshape(cells_x, cells_y, deep * 8, 256)
    table = jnp.pad(rel_bias * 1.4426950408889634, ((0, 8 - heads), (0, TABLE - rel_bias.shape[1])))
    bias = expand_table(table, heads)
    wside, wtrans = side_weights(w_qkv, b_qkv, heads)
    gain = jnp.broadcast_to(layer_norm_gain[:, None], (feats, LANES))
    shift = jnp.broadcast_to(layer_norm_bias[:, None], (feats, LANES))
    flags = jnp.stack(
        [(lax.axis_index(a) == lax.axis_size(a) - 1).astype(F32) for a in ("gx", "gy", "gz")]
    )
    d_x, pairs, gq, gkv, gproj, vec = window_call(
        flags, xd, bias, gain, shift, wside, wtrans, w_proj, w_qkv[:, :feats], w_qkv[:, feats:], heads
    )
    d_x = d_x.reshape(cells_x, cells_y, deep, 8, feats)[:, :, :, :WIN].reshape(inputs.shape)
    for dim, axis in enumerate(("gx", "gy", "gz")):
        d_x = backward(d_x, dim, axis)
    rel = fold_table(pairs)[:heads]
    vec = jnp.sum(vec, -1)
    both = jnp.concatenate([gq, gkv], 1)
    count = inputs.shape[0] * inputs.shape[1] * inputs.shape[2]
    for a in ("gx", "gy", "gz"):
        count *= lax.axis_size(a)
    totals = lax.psum((both, gproj, rel, vec), ("gx", "gy", "gz"))
    both, gproj, rel, vec = [t * float(count) ** (-0.5) for t in totals]
    return (
        d_x, both[:feats], both[feats], gproj, rel[:, : rel_bias.shape[1]], vec[0], vec[1],
    )


def solution(mesh):
    placed = (P("gx", "gy", "gz", None), P("gx", "gy", "gz", None), P(), P(), P(), P(), P(), P())
    return jax.shard_map(
        shards,
        mesh=mesh,
        in_specs=placed,
        out_specs=(P("gx", "gy", "gz", None), P(), P(), P(), P(), P(), P()),
        check_vma=False,
    )
```

time: 706 us -> 349 us (0.49)
  matrix products: 211 us -> 0 us
  local copies, waits for them, and re-layouts: 203 us -> 33.1 us
  Pallas kernels: 0 us -> 84.3 us
  other arithmetic: 73.7 us -> 26.2 us
  starting transfers between devices: 26.1 us -> 12.4 us
  waiting for transfers between devices: 125 us -> 138 us
    dot_general x46 -> x0, matrix products: 183 us -> none  [the longest x1 71.1 us: expand_table(): section = jnp.einsum('hxbcBC,aAx->habcABC', section, ones, precision=exact)]
    pallas_call x0 -> x3, Pallas kernels: none -> 84.3 us  [the longest x1 70.3 us: window_call(): pl.pallas_call(window_body, grid=grid, in_specs=[pl.BlockSpec(memory_spac...]
    reshape x4 -> x2, local copies, waits for them, and re-layouts: 80.1 us -> 3.2 us  [the longest x1 2.38 us: shards(): jnp.pad(xd, ((0, 0), (0, 0), (0, 0), (0, 1), (0, 0)))]
    unnamed x51 -> x33, local copies, waits for them, and re-layouts: 67.5 us -> 1.63 us
    reduce_sum x14 -> x1, other arithmetic: 32.2 us -> 0.11 us  [shards(): vec = jnp.sum(vec, -1)]
    sub x4 -> x0, matrix products: 27.8 us -> none  [window_pass(): expo = jnp.exp(scores - top)]
    ppermute x6, waiting for transfers between devices: 3.95 us -> 27.3 us  [shifted(): return lax.ppermute(block, axis, route)]
    add x1 -> x0, local copies, waits for them, and re-layouts: 20.9 us -> none  [window_pass(): jnp.einsum('ghid,ghjd->ghij', query, keys, preferred_element_type=f32)]
  transfers between devices with their start and end apart: 7 -> 7, of which waited for: 2 -> 5; matrix products, arithmetic and copies ran while one was open for 43% -> 11% of each run, Pallas kernels for 0% -> 2%
where the time goes in v1:
time: 349 us; the launch traced here: 347 us
  waiting for transfers between devices  138 us (40%)
  Pallas kernels  84.3 us (24%)
  blocking collectives  38.5 us (11%)
  local copies, waits for them, and re-layouts  33.1 us (9%)
  other arithmetic  26.2 us (8%)
  between operations  14.3 us (4%)
  starting transfers between devices  12.4 us (4%)
    psum x1, waiting for transfers between devices, shards(): totals = lax.psum((both, gproj, rel, vec), ('gx', 'gy', 'gz'))  111 us
    pallas_call x1, Pallas kernels, window_call(): pl.pallas_call(window_body, grid=grid, in_specs=[pl.BlockSpec(memory_spac...  70.3 us
    psum x1, blocking collectives, shards(): totals = lax.psum((both, gproj, rel, vec), ('gx', 'gy', 'gz'))  38.5 us
    ppermute x6, waiting for transfers between devices, shifted(): return lax.ppermute(block, axis, route)  27.3 us
    ppermute x6, starting transfers between devices, shifted(): return lax.ppermute(block, axis, route)  12.4 us
    pallas_call x1, Pallas kernels, expand_table(): pl.pallas_call(expand_body, out_shape=jax.ShapeDtypeStruct((heads, ROWS,...  7.61 us
  transfers between devices with their start and end apart: 7, of which 5 were waited for; matrix products, arithmetic and copies ran while one was open for 11% of the time, Pallas kernels for 2%

profile of v1, /device:TPU:0, one launch (start us, length us, event | category | flops | bytes accessed | tf_op | source)
XLA Modules:
  0.0 346.8 jit_solution(5882554251164325584)
XLA Ops:
  7.5 2.1 pad_maximum_fusion.5
  9.6 5.1 %collective-permute-start = (bf16[3,28,7,256]{3,2,1,0:T(8,128)(2,1)}, bf16[3,28,7,256]{3,2,1,0:T(8,128)(2,1)S(1)}, u32[]{:S(2)}, u32[]{:S(2)}) collective-permute-start(bf16[3,28,7,256]{3,2,1,0:T(8,128)(2,1)} %pad_maximum_fusion.5), channel_id=1, source_target_pairs={{8,0},{16,8},{24,16},{0,24},{9,1},{17,9},{25,17},{1,25},{10,2},{18... | collective-permute-start | bytes 903176 | tf_op jit(solution)/shard_map/ppermute | solution.py:346
  16.8 0.7 broadcast_in_dim.51
  17.5 1.5 concatenate.66
  19.1 1.4 broadcast_in_dim.50
  20.5 1.5 concatenate.65
  22.0 1.4 broadcast_in_dim.49
  23.4 1.5 concatenate.64
  25.0 5.0 %pad_maximum_fusion = bf16[28,28,7,256]{3,2,1,0:T(8,128)(2,1)} fusion(bf16[28,28,7,32]{3,2,1,0:T(8,128)(2,1)S(1)} %broadcast_in_dim.39, bf16[28,28,7,96]{3,2,1,0:T(8,128)(2,1)S(1)} %copy-done.1, bf16[28,28,7,96]{3,2,1,0:T(8,128)(2,1)} %param.8), kind=kLoop, calls=%fused_computation | loop fusion | flops 11239424 | bytes 5268480 | tf_op jit(solution)/shard_map/concatenate | solution.py:364
  30.0 0.6 broadcast_multiply_fusion.2
  30.6 1.0 copy.30
  31.6 1.1 concatenate.55
  33.4 1.1 concatenate.58
  35.1 1.3 and_convert_fusion
  36.5 2.0 slice.104
  38.6 1.0 maximum_maximum_fusion
  39.7 0.7 collective-permute-start.1
  41.0 2.3 fusion
  43.3 1.8 collective-permute-done.1
  45.8 1.4 copy.28
  47.2 1.5 collective-permute-start.2
  49.9 0.7 slice.89.wkv_ref
  50.6 0.8 copy.38.wside_ref
  51.4 1.4 pad.9.table_ref
  52.8 1.4 pad_maximum_fusion.8.wtrans_ref
  54.2 7.6 %expand.1.bias_ref = f32[3,344,384]{2,1,0:T(8,128)} custom-call(f32[8,2304]{1,0:T(8,128)} %pad.9.table_ref), custom_call_target="tpu_custom_call" | custom-call | flops 8999999488 | bytes 2000000 | tf_op jit(solution)/shard_map/expand/pallas_call | solution.py:93
  61.9 1.5 fusion.1
  63.3 17.0 %collective-permute-done.2 = bf16[28,28,3,256]{3,1,2,0:T(8,128)(2,1)} collective-permute-done((bf16[28,28,3,256]{3,1,2,0:T(8,128)(2,1)}, bf16[28,28,3,256]{3,1,2,0:T(8,128)(2,1)}, u32[]{:S(2)}, u32[]{:S(2)}) %collective-permute-start.2) | collective-permute-done | bytes 1204256 | tf_op jit(solution)/shard_map/ppermute | solution.py:346
  80.4 2.5 copy.29
  82.8 1.7 maximum_bitcast_fusion
  84.5 2.4 pad_bitcast_fusion.xd_ref
  86.9 0.7 broadcast_in_dim.40.gain_ref
  87.7 0.8 broadcast_in_dim.41.shift_ref
  88.4 70.3 %windows.1 = (bf16[28,28,8,96]{3,2,1,0:T(8,128)(2,1)}, f32[3,344,384]{2,1,0:T(8,128)}, f32[112,96]{1,0:T(8,128)}, f32[112,192]{1,0:T(8,128)}, f32[96,96]{1,0:T(8,128)}, /*index=5*/f32[2,96,384]{2,1,0:T(8,128)}) custom-call(f32[3]{0:T(128)} %add_convert_fusion.flag_ref, bf16[28,28,8,256]{3,2,1,0:T(8,128)(2,1)} %pad_bitcast_fusion.xd_ref, ...), custom_call_target="tpu_custom_call" | custom-call | tf_op jit(solution)/shard_map/windows/pallas_call | solution.py:295
  158.8 1.0 slice_bitcast_fusion.1
  159.8 1.5 slice_bitcast_fusion
  161.3 6.3 %fold.1 = f32[8,2304]{1,0:T(8,128)} custom-call(f32[3,344,384]{2,1,0:T(8,128)} %get-tuple-element.17.pairs_ref), custom_call_target="tpu_custom_call" | custom-call | tf_op jit(solution)/shard_map/fold/pallas_call | solution.py:128
  167.7 0.9 slice.118
  168.6 38.5 %all-reduce.2 = (f32[96,96]{1,0:T(8,128)S(1)}, f32[3,2304]{1,0:T(4,128)S(1)}, f32[2,96]{1,0:T(2,128)S(1)}) all-reduce(f32[96,96]{1,0:T(8,128)S(1)} %copy-done.9, f32[3,2304]{1,0:T(4,128)S(1)} %slice.118, f32[2,96]{1,0:T(2,128)S(1)} %reduce_sum.9), channel_id=1, replica_groups=mesh['gx'=4,'gy'=4,'gz'=2] {'gx','gy','gz'}, use_global_device_ids=true, to_apply=%region_1.2 | all-reduce | flops 16320 | bytes 130560 | tf_op jit(solution)/shard_map/psum | solution.py:390
  208.3 2.9 collective-permute-start.3
  211.2 0.8 pad_maximum_fusion.7
  212.0 3.5 %collective-permute-done.3 = bf16[3,28,7,96]{3,2,1,0:T(8,128)(2,1)S(1)} collective-permute-done((bf16[3,28,7,96]{3,2,1,0:T(8,128)(2,1)S(1)}, bf16[3,28,7,96]{3,2,1,0:T(8,128)(2,1)S(1)}, u32[]{:S(2)}, u32[]{:S(2)}) %collective-permute-start.3) | collective-permute-done | bytes 112928 | tf_op jit(solution)/shard_map/ppermute | solution.py:346
  215.6 5.0 %collective-permute-done.4 = bf16[28,3,7,96]{3,2,1,0:T(8,128)(2,1)S(1)} collective-permute-done((bf16[28,3,7,96]{3,2,1,0:T(8,128)(2,1)S(1)}, bf16[28,3,7,96]{3,2,1,0:T(8,128)(2,1)S(1)}, u32[]{:S(2)}, u32[]{:S(2)}) %collective-permute-start.4) | collective-permute-done | bytes 112928 | tf_op jit(solution)/shard_map/ppermute | solution.py:346
  221.6 2.2 collective-permute-start.5
  224.3 110.6 %all-reduce.5.cloned.1.call-done = f32[112,288]{1,0:T(8,128)} async-done(((f32[112,288]{1,0:T(8,128)}), f32[112,288]{1,0:T(8,128)}) %all-reduce.5.cloned.1.call-update) | async-done | bytes 129040 | tf_op jit(solution)/shard_map/psum | solution.py:390
  334.9 0.9 broadcast_multiply_fusion
  335.8 0.7 slice.116
  337.8 2.2 pad_maximum_fusion.3
  (66 shorter events, 10.6 us)
Async XLA Ops:
  7.2 327.7 %all-reduce.5.cloned.1.call-start = ((), (), s32[]{:S(2)}) async-start(), calls=%async_computation | async-start | bytes 344064 | tf_op jit(solution)/shard_map/psum | solution.py:390
  7.4 8.2 %copy-start.13 = (f32[288]{0:T(512)S(1)}, f32[288]{0:T(512)}, u32[]{:S(2)}) copy-start(f32[288]{0:T(512)} %param.13) | copy-start | bytes 3460
  7.4 17.5 %copy-start.1 = (bf16[28,28,7,96]{3,2,1,0:T(8,128)(2,1)S(1)}, bf16[28,28,7,96]{3,2,1,0:T(8,128)(2,1)}, u32[]{:S(2)}) copy-start(bf16[28,28,7,96]{3,2,1,0:T(8,128)(2,1)} %param.9) | copy-start | bytes 3161092
  9.6 30.0 %collective-permute-start = (bf16[3,28,7,256]{3,2,1,0:T(8,128)(2,1)}, bf16[3,28,7,256]{3,2,1,0:T(8,128)(2,1)S(1)}, u32[]{:S(2)}, u32[]{:S(2)}) collective-permute-start(bf16[3,28,7,256]{3,2,1,0:T(8,128)(2,1)} %pad_maximum_fusion.5), channel_id=1, source_target_pairs={{8,0},{16,8},{24,16},{0,24},{9,1},{17,9},{25,17},{1,25},{10,2},{18... | collective-permute-start | bytes 903176 | tf_op jit(solution)/shard_map/ppermute | solution.py:346
  16.2 0.6 copy-start.12
  25.0 5.0 %copy-start.10 = (f32[3,2197]{1,0:T(4,128)S(1)}, f32[3,2197]{1,0:T(4,128)}, u32[]{:S(2)}) copy-start(f32[3,2197]{1,0:T(4,128)} %param.15) | copy-start | bytes 79096
  38.5 1.9 copy-start
  38.5 1.9 copy-start.11
  38.5 1.9 copy-start.7
  39.7 5.5 %collective-permute-start.1 = (bf16[28,3,7,256]{3,2,1,0:T(8,128)(2,1)S(1)}, bf16[28,3,7,256]{3,2,1,0:T(8,128)(2,1)S(1)}, u32[]{:S(2)}, u32[]{:S(2)}) collective-permute-start(bf16[28,3,7,256]{3,2,1,0:T(8,128)(2,1)S(1)} %pad_maximum_fusion.4), channel_id=1, source_target_pairs={{2,0},{4,2},{6,4},{0,6},{3,1},{5,3},{7,5},{1,7},{10,8},{12,10},{14... | collective-permute-start | bytes 903176 | tf_op jit(solution)/shard_map/ppermute | solution.py:346
  43.3 6.0 %copy-start.4 = (bf16[96,288]{1,0:T(8,128)(2,1)S(1)}, bf16[96,288]{1,0:T(8,128)(2,1)}, u32[]{:S(2)}) copy-start(bf16[96,288]{1,0:T(8,128)(2,1)} %param.12) | copy-start | bytes 165892
  43.3 7.3 %copy-start.2 = (bf16[128,2,3,128]{0,3,2,1:T(8,128)(2,1)S(1)}, bf16[128,2,3,128]{0,3,2,1:T(8,128)(2,1)}, u32[]{:S(2)}) copy-start(bf16[128,2,3,128]{0,3,2,1:T(8,128)(2,1)} %maximum_maximum_fusion) | copy-start | bytes 589828
  45.8 7.1 %copy-start.5 = (bf16[192,112]{1,0:T(8,128)(2,1)S(1)}, bf16[192,112]{1,0:T(8,128)(2,1)}, u32[]{:S(2)}) copy-start(bf16[192,112]{1,0:T(8,128)(2,1)} %slice_bitcast_fusion.2) | copy-start | bytes 129028
  47.2 33.2 %collective-permute-start.2 = (bf16[28,28,3,256]{3,1,2,0:T(8,128)(2,1)}, bf16[28,28,3,256]{3,1,2,0:T(8,128)(2,1)}, u32[]{:S(2)}, u32[]{:S(2)}) collective-permute-start(bf16[28,28,3,256]{3,1,2,0:T(8,128)(2,1)} %copy.28), channel_id=1, source_target_pairs={{1,0},{0,1},{3,2},{2,3},{5,4},{4,5},{7,6},{6,7},{9,8},{8,9},{11,10... | collective-permute-start | bytes 3612680 | tf_op jit(solution)/shard_map/ppermute | solution.py:346
  84.5 2.4 copy-start.14
  84.5 3.1 copy-start.15
  158.7 2.5 copy-start.3
  158.7 9.8 %copy-start.9 = (f32[96,96]{1,0:T(8,128)S(1)}, f32[96,96]{1,0:T(8,128)}, u32[]{:S(2)}) copy-start(f32[96,96]{1,0:T(8,128)} %get-tuple-element.16) | copy-start | bytes 110596
  158.8 52.4 %copy-start.6 = (f32[112,192]{1,0:T(8,128)S(1)}, f32[112,192]{1,0:T(8,128)}, u32[]{:S(2)}) copy-start(f32[112,192]{1,0:T(8,128)} %get-tuple-element.15) | copy-start | bytes 258052
  158.8 52.4 %copy-start.8 = (f32[112,96]{1,0:T(8,128)S(1)}, f32[112,96]{1,0:T(8,128)}, u32[]{:S(2)}) copy-start(f32[112,96]{1,0:T(8,128)} %get-tuple-element.14) | copy-start | bytes 129028
  208.3 7.2 %collective-permute-start.3 = (bf16[3,28,7,96]{3,2,1,0:T(8,128)(2,1)S(1)}, bf16[3,28,7,96]{3,2,1,0:T(8,128)(2,1)S(1)}, u32[]{:S(2)}, u32[]{:S(2)}) collective-permute-start(bf16[3,28,7,96]{3,2,1,0:T(8,128)(2,1)S(1)} %slice_bitcast_fusion.1), channel_id=1, source_target_pairs={{24,0},{0,8},{8,16},{16,24},{25,1},{1,9},{9,17},{17,25},{26,2},{2,... | collective-permute-start | bytes 338696 | tf_op jit(solution)/shard_map/ppermute | solution.py:346
  215.6 5.0 %collective-permute-start.4 = (bf16[28,3,7,96]{3,2,1,0:T(8,128)(2,1)S(1)}, bf16[28,3,7,96]{3,2,1,0:T(8,128)(2,1)S(1)}, u32[]{:S(2)}, u32[]{:S(2)}) collective-permute-start(bf16[28,3,7,96]{3,2,1,0:T(8,128)(2,1)S(1)} %pad_maximum_fusion.6), channel_id=1, source_target_pairs={{6,0},{0,2},{2,4},{4,6},{7,1},{1,3},{3,5},{5,7},{14,8},{8,10},{10,... | collective-permute-start | bytes 338696 | tf_op jit(solution)/shard_map/ppermute | solution.py:346
  221.6 115.7 %collective-permute-start.5 = (bf16[28,28,3,96]{3,1,2,0:T(8,128)(2,1)S(1)}, bf16[28,28,3,96]{3,1,2,0:T(8,128)(2,1)S(1)}, u32[]{:S(2)}, u32[]{:S(2)}) collective-permute-start(bf16[28,28,3,96]{3,1,2,0:T(8,128)(2,1)S(1)} %copy.39), channel_id=1, source_target_pairs={{1,0},{0,1},{3,2},{2,3},{5,4},{4,5},{7,6},{6,7},{9,8},{8,9},{11,10... | collective-permute-start | bytes 1354760 | tf_op jit(solution)/shard_map/ppermute | solution.py:346
Sparse Core Ops, SparseCore 0:
  212.1 122.7 all-reduce.4

commit v2 on v1

--- a/solution.py
+++ b/solution.py
@@ -17,6 +17,7 @@
 WIDE = 1152
 TABLE = 2304
 HID = 112
+REL_AT = 104
 AUG = 80
 BIG = 1e30
 F32 = jnp.float32
@@ -71,7 +72,36 @@
     return (WIN - 1 - first) * SPAN * SPAN + (WIN - 1 - second) * SPAN
 
 
-def expand_body(table_ref, bias_ref, base_ref, ones_ref, wide_ref):
+def slab_token(place):
+    third = place & 7
+    third = third + (WIN - SHIFT) - jnp.where(third >= SHIFT, WIN, 0)
+    return jnp.where((place & 7) == 7, -1, (place >> 3) * WIN + third)
+
+
+def expand_body(table_ref, bias_ref, pack_ref, unpack_ref, kmask_ref, qmask_ref, base_ref, ones_ref, wide_ref):
+    place = lax.broadcasted_iota(jnp.int32, (LANES, SLAB), 1)
+    token = lax.broadcasted_iota(jnp.int32, (LANES, SLAB), 0)
+    pack_ref[...] = jnp.where(token == slab_token(place), 1.0, 0.0).astype(BF16)
+    place = lax.broadcasted_iota(jnp.int32, (SLAB, LANES), 0)
+    token = lax.broadcasted_iota(jnp.int32, (SLAB, LANES), 1)
+    unpack_ref[...] = jnp.where(token == slab_token(place), 1.0, 0.0).astype(BF16)
+    row = lax.broadcasted_iota(jnp.int32, (ROWS, 128), 0)
+    lane = lax.broadcasted_iota(jnp.int32, (ROWS, 128), 1)
+    late = [(part >= WIN - SHIFT).astype(F32) for part in places(row)]
+    value = jnp.zeros((ROWS, 128), F32)
+    for axis in range(3):
+        value = jnp.where(lane == 64 + 2 * axis, -BIG * (1.0 - late[axis]), value)
+        value = jnp.where(lane == 65 + 2 * axis, -BIG * late[axis], value)
+    value = jnp.where((lane == 70) & (row >= TOK), -BIG, value)
+    kmask_ref[...] = value
+    row = lax.broadcasted_iota(jnp.int32, (16, LANES), 0)
+    lane = lax.broadcasted_iota(jnp.int32, (16, LANES), 1)
+    late = [(part >= WIN - SHIFT).astype(F32) for part in places(lane)]
+    value = jnp.where(row == 6, 1.0, 0.0)
+    for axis in range(3):
+        value = jnp.where(row == 2 * axis, late[axis], value)
+        value = jnp.where(row == 2 * axis + 1, 1.0 - late[axis], value)
+    qmask_ref[...] = value.astype(BF16)
     ones_ref[...] = spread_ones()
     heads = bias_ref.shape[0]
     for head in range(heads):
@@ -92,22 +122,39 @@
 def expand_table(table, heads, interpret=False):
     return pl.pallas_call(
         expand_body,
-        out_shape=jax.ShapeDtypeStruct((heads, ROWS, LANES), F32),
+        out_shape=[
+            jax.ShapeDtypeStruct((heads, ROWS, LANES), F32),
+            jax.ShapeDtypeStruct((LANES, SLAB), BF16),
+            jax.ShapeDtypeStruct((SLAB, LANES), BF16),
+            jax.ShapeDtypeStruct((ROWS, 128), F32),
+            jax.ShapeDtypeStruct((16, LANES), BF16),
+        ],
         scratch_shapes=[
             pltpu.VMEM((8, TABLE), F32),
             pltpu.VMEM((WIDE, LANES), BF16),
             pltpu.VMEM((SLAB, WIDE), F32),
         ],
-        cost_estimate=pl.CostEstimate(flops=9_000_000_000, bytes_accessed=2_000_000, transcendentals=0),
+        cost_estimate=pl.CostEstimate(flops=4_000_000_000, bytes_accessed=2_000_000, transcendentals=0),
         interpret=interpret,
         name="expand",
     )(table)
 
 
-def fold_body(pairs_ref, table_ref, rows_ref, ones_ref, total_ref):
+def column_sums(value):
+    part = value[:, :128] + value[:, 128:256] + value[:, 256:]
+    part = jnp.concatenate([part, jnp.zeros((128 - part.shape[0], 128), F32)], 0)
+    return jnp.sum(part.T, 0, keepdims=True)
+
+
+def fold_body(pairs_ref, gq_ref, gkv_ref, gproj_ref, vec_ref, out_ref, rows_ref, ones_ref, total_ref):
     ones_ref[...] = spread_ones()
     heads = pairs_ref.shape[0]
-    table_ref[...] = jnp.zeros(table_ref.shape, F32)
+    feats = gproj_ref.shape[0]
+    out_ref[...] = jnp.zeros(out_ref.shape, F32)
+    proj = jnp.concatenate([gproj_ref[...], jnp.zeros((8, feats), F32)], 0)
+    out_ref[:REL_AT, :] = jnp.concatenate([gq_ref[:REL_AT], gkv_ref[:REL_AT], proj], 1)
+    for at in range(2):
+        out_ref[feats + 1 + at : feats + 2 + at, :128] = column_sums(vec_ref[at])
     rows_ref[...] = jnp.zeros(rows_ref.shape, F32)
     for head in range(heads):
         for group in range(WIN * WIN):
@@ -120,68 +167,104 @@
                 at = offset_of(first, second)
                 rows = 8 * (first * WIN + second)
                 total_ref[:, at : at + WIDE] = total_ref[:, at : at + WIDE] + wide[rows : rows + 8]
-        sheared = shear(total_ref[...], 1)
-        table_ref[head : head + 1, :] = jnp.sum(sheared, 0, keepdims=True)
-
-
-def fold_table(pairs, interpret=False):
+        entries = jnp.sum(shear(total_ref[...], 1), 0, keepdims=True)
+        for part in range(TABLE // LANES):
+            row = REL_AT + head * (TABLE // LANES) + part
+            out_ref[row : row + 1, :] = entries[:, LANES * part : LANES * part + LANES]
+
+
+def fold_sums(sums, interpret=False):
     return pl.pallas_call(
         fold_body,
-        out_shape=jax.ShapeDtypeStruct((8, TABLE), F32),
+        out_shape=jax.ShapeDtypeStruct((128, LANES), F32),
         scratch_shapes=[
             pltpu.VMEM((SLAB, LANES), F32),
             pltpu.VMEM((WIDE, LANES), BF16),
             pltpu.VMEM((8, TABLE), F32),
         ],
+        cost_estimate=pl.CostEstimate(flops=3_000_000_000, bytes_accessed=2_000_000, transcendentals=0),
         interpret=interpret,
         name="fold",
-    )(pairs)
-
-
-def window_body(
-    flag_ref, xd_ref, bias_ref, gain_ref, shift_ref, wside_ref, wtrans_ref, wproj_ref, wq_ref, wkv_ref,
-    dx_ref, pair_ref, gq_ref, gkv_ref, gproj_ref, vec_ref,
-    pack_ref, unpack_ref, kmask_ref, qmask_ref, score_ref, expo_ref, grad_ref, qdiag_ref, odiag_ref,
-    kaug_ref, vaug_ref, attn_ref, dq_ref,
-):
+    )(*sums)
+
+
+def gather(x_ref, d_ref, yhalo_ref, xhalo_ref, zhalo_ref, block_ref, base, last):
+    feats = x_ref.shape[3]
+    row, col = pl.program_id(0), pl.program_id(1)
+    at_x = WIN * (row + base) + SHIFT
+    at_y = WIN * col + SHIFT
+    edge = WIN - SHIFT
+    last_col = col == pl.num_programs(1) - 1
+
+    def own(first, count_x, second, count_y):
+        spot = (pl.ds(at_x + first, count_x), pl.ds(at_y + second, count_y))
+        here = (slice(first, first + count_x), slice(second, second + count_y), slice(0, WIN))
+        block_ref[here + (slice(0, feats),)] = x_ref[spot].astype(F32)
+        block_ref[here + (slice(128, 128 + feats),)] = d_ref[spot].astype(F32)
+
+    def arrived(first, count_x):
+        block_ref[first : first + count_x, edge:, :WIN, :] = yhalo_ref[pl.ds(at_x + first, count_x)].astype(F32)
+
+    def rows(first, count_x):
+        own(first, count_x, 0, edge)
+
+        @pl.when(last_col)
+        def _():
+            arrived(first, count_x)
+
+        @pl.when(jnp.logical_not(last_col))
+        def _():
+            own(first, count_x, edge, SHIFT)
+
+    if xhalo_ref is None:
+        rows(0, WIN)
+    else:
+        last_row = row == pl.num_programs(0) - 1
+        rows(0, edge)
+
+        @pl.when(last_row)
+        def _():
+            block_ref[edge:, :, :WIN, :] = xhalo_ref[:, pl.ds(WIN * col, WIN)].astype(F32)
+
+        @pl.when(jnp.logical_not(last_row))
+        def _():
+            rows(edge, SHIFT)
+
+    block_ref[:, :, :SHIFT, :] = zhalo_ref[pl.ds(WIN * row, WIN), pl.ds(WIN * col, WIN)].astype(F32)
+
+
+def window_body(base, has_xhalo, has_sums, *refs):
+    refs = list(refs)
+    flag_ref, x_ref, d_ref, yhalo_ref, zhalo_ref = refs[:5]
+    refs = refs[5:]
+    xhalo_ref = refs.pop(0) if has_xhalo else None
+    bias_ref, pack_ref, unpack_ref, kmask_ref, qmask_ref = refs[:5]
+    gain_ref, shift_ref, wside_ref, wtrans_ref, wproj_ref, wqkv_ref = refs[5:11]
+    refs = refs[11:]
+    before = [refs.pop(0) for _ in range(5)] if has_sums else None
+    dx_ref, pair_ref, gq_ref, gkv_ref, gproj_ref, vec_ref = refs[:6]
+    (block_ref, score_ref, expo_ref, grad_ref, qdiag_ref, odiag_ref, kaug_ref, vaug_ref, attn_ref, dq_ref) = refs[6:]
+    sums = (pair_ref, gq_ref, gkv_ref, gproj_ref, vec_ref)
     heads = pair_ref.shape[0]
     feats = wproj_ref.shape[0]
     hdim = feats // heads
     scale = hdim ** (-0.5)
-    at = [pl.program_id(axis) for axis in range(3)]
-    first_step = (at[0] == 0) & (at[1] == 0) & (at[2] == 0)
-
-    @pl.when(first_step)
+    row, col = pl.program_id(0), pl.program_id(1)
+    last = [
+        ((row == pl.num_programs(0) - 1) if has_xhalo else False),
+        col == pl.num_programs(1) - 1,
+        True,
+    ]
+
+    @pl.when((row == 0) & (col == 0))
     def _():
-        place = lax.broadcasted_iota(jnp.int32, (LANES, SLAB), 1)
-        token = lax.broadcasted_iota(jnp.int32, (LANES, SLAB), 0)
-        target = jnp.where((place & 7) == 7, -1, place - (place >> 3))
-        pack_ref[...] = jnp.where(token == target, 1.0, 0.0).astype(BF16)
-        place = lax.broadcasted_iota(jnp.int32, (SLAB, LANES), 0)
-        token = lax.broadcasted_iota(jnp.int32, (SLAB, LANES), 1)
-        target = jnp.where((place & 7) == 7, -1, place - (place >> 3))
-        unpack_ref[...] = jnp.where(token == target, 1.0, 0.0).astype(BF16)
-        row = lax.broadcasted_iota(jnp.int32, (ROWS, 128), 0)
-        lane = lax.broadcasted_iota(jnp.int32, (ROWS, 128), 1)
-        late = [(part >= WIN - SHIFT).astype(F32) for part in places(row)]
-        value = jnp.zeros((ROWS, 128), F32)
-        for axis in range(3):
-            value = jnp.where(lane == 64 + 2 * axis, -BIG * (1.0 - late[axis]), value)
-            value = jnp.where(lane == 65 + 2 * axis, -BIG * late[axis], value)
-        value = jnp.where((lane == 70) & (row >= TOK), -BIG, value)
-        kmask_ref[...] = value
-        row = lax.broadcasted_iota(jnp.int32, (16, LANES), 0)
-        lane = lax.broadcasted_iota(jnp.int32, (16, LANES), 1)
-        late = [(part >= WIN - SHIFT).astype(F32) for part in places(lane)]
-        value = jnp.where(row == 6, 1.0, 0.0)
-        for axis in range(3):
-            value = jnp.where(row == 2 * axis, late[axis], value)
-            value = jnp.where(row == 2 * axis + 1, 1.0 - late[axis], value)
-        qmask_ref[...] = value.astype(BF16)
-        for ref in (pair_ref, gq_ref, gkv_ref, gproj_ref, vec_ref, qdiag_ref, odiag_ref):
+        for at, ref in enumerate(sums):
+            ref[...] = jnp.zeros(ref.shape, ref.dtype) if before is None else before[at][...]
+        for ref in (block_ref, qdiag_ref, odiag_ref):
             ref[...] = jnp.zeros(ref.shape, ref.dtype)
 
-    block = xd_ref[...].astype(F32).reshape(SLAB, 256).astype(BF16)
+    gather(x_ref, d_ref, yhalo_ref, xhalo_ref, zhalo_ref, block_ref, base, last)
+    block = block_ref[...].reshape(SLAB, 256).astype(BF16)
     packed = dot(pack_ref[...], block)
     dy_tok = packed[:, 128:].astype(BF16)
     x_t = packed[:, :128].T[:feats]
@@ -201,8 +284,8 @@
     lane = lax.broadcasted_iota(jnp.int32, (1, 128), 1)
     flags = jnp.where(lane == 70, 1.0, 0.0)
     for axis in range(3):
-        last = (at[axis] == pl.num_programs(axis) - 1).astype(F32) * flag_ref[axis]
-        flags = jnp.where((lane == 64 + 2 * axis) | (lane == 65 + 2 * axis), last, flags)
+        edge = jnp.where(last[axis], flag_ref[axis], 0.0)
+        flags = jnp.where((lane == 64 + 2 * axis) | (lane == 65 + 2 * axis), edge, flags)
     kmask = kmask_ref[...] * flags
     ones = jnp.where((lane >= 64) & (lane < 67), 1.0, 0.0)
     side = dot(norm_tok, wside_ref[...])
@@ -259,7 +342,7 @@
     gkv_ref[...] = gkv_ref[...] + dot(norm_t[:, :ROWS], dkv)
     gproj_ref[...] = gproj_ref[...] + dot(attn_ref[...], dy_tok[:, :feats])
     dkv_all = jnp.concatenate([dkv, jnp.zeros((LANES - ROWS, 2 * feats), BF16)], 0)
-    grad_in = dot(wq_ref[...], dq) + dot(wkv_ref[...], dkv_all, NT)
+    grad_in = dot(wqkv_ref[:, :feats], dq) + dot(wqkv_ref[:, feats:], dkv_all, NT)
     vec_ref[0] = vec_ref[0] + grad_in * xhat
     vec_ref[1] = vec_ref[1] + grad_in
     dhat = grad_in * gain_ref[...]
@@ -270,40 +353,26 @@
     dx_ref[...] = spread.reshape(WIN, WIN, 8, feats).astype(BF16)
 
 
-def window_call(flags, xd, bias, gain, shift, wside, wtrans, wproj, wq, wkv, heads, interpret=False):
-    feats = wproj.shape[0]
-    grid = (xd.shape[0] // WIN, xd.shape[1] // WIN, xd.shape[2] // 8)
+def window_call(base, count, flags, own, yhalo, zhalo, xhalo, tables, weights, sums, heads, interpret=False):
+    cells_x, cells_y, cells_z, feats = own[0].shape
+    grid = (count, cells_y // WIN)
 
     def whole(array):
         zeros = (0,) * array.ndim
         return pl.BlockSpec(array.shape, lambda *_: zeros)
 
-    def total(shape):
-        zeros = (0,) * len(shape)
-        return pl.BlockSpec(shape, lambda *_: zeros), jax.ShapeDtypeStruct(shape, F32)
-
-    def tile(width):
-        return pl.BlockSpec((WIN, WIN, 8, width), lambda i, j, k: (i, j, k, 0))
-
-    sums = [
-        total((heads, ROWS, LANES)),
-        total((HID, feats)),
-        total((HID, 2 * feats)),
-        total((feats, feats)),
-        total((2, feats, LANES)),
-    ]
+    arrays = list(own) + [yhalo, zhalo] + ([] if xhalo is None else [xhalo])
+    arrays += list(tables) + list(weights) + ([] if sums is None else list(sums))
+    shapes = [(heads, ROWS, LANES), (HID, feats), (HID, 2 * feats), (feats, feats), (2, feats, LANES)]
+    shapes = [jax.ShapeDtypeStruct(shape, F32) for shape in shapes]
     return pl.pallas_call(
-        window_body,
+        functools.partial(window_body, base, xhalo is not None, sums is not None),
         grid=grid,
-        in_specs=[pl.BlockSpec(memory_space=pltpu.SMEM), tile(256)]
-        + [whole(a) for a in (bias, gain, shift, wside, wtrans, wproj, wq, wkv)],
-        out_specs=[tile(feats)] + [s[0] for s in sums],
-        out_shape=[jax.ShapeDtypeStruct(xd.shape[:3] + (feats,), BF16)] + [s[1] for s in sums],
+        in_specs=[pl.BlockSpec(memory_space=pltpu.SMEM)] + [whole(a) for a in arrays],
+        out_specs=[pl.BlockSpec((WIN, WIN, 8, feats), lambda i, j: (i, j, 0, 0))] + [whole(s) for s in shapes],
+        out_shape=[jax.ShapeDtypeStruct((WIN * count, cells_y, 8, feats), BF16)] + shapes,
         scratch_shapes=[
-            pltpu.VMEM((LANES, SLAB), BF16),
-            pltpu.VMEM((SLAB, LANES), BF16),
-            pltpu.VMEM((ROWS, 128), F32),
-            pltpu.VMEM((16, LANES), BF16),
+            pltpu.VMEM((WIN, WIN, 8, 256), F32),
             pltpu.VMEM((ROWS, LANES), F32),
             pltpu.VMEM((ROWS, heads * LANES), BF16),
             pltpu.VMEM((ROWS, heads * LANES), BF16),
@@ -315,11 +384,14 @@
             pltpu.VMEM((feats, LANES), BF16),
         ],
         compiler_params=pltpu.CompilerParams(
-            dimension_semantics=("arbitrary",) * 3, vmem_limit_bytes=60 * 1024 * 1024
+            dimension_semantics=("arbitrary",) * 2, vmem_limit_bytes=56 * 1024 * 1024
+        ),
+        cost_estimate=pl.CostEstimate(
+            flops=2_200_000_000 * count * grid[1], bytes_accessed=8_000_000, transcendentals=0
         ),
         interpret=interpret,
         name="windows",
-    )(flags, xd, bias, gain, shift, wside, wtrans, wproj, wq, wkv)
+    )(flags, *arrays)
 
 
 def side_weights(w_qkv, b_qkv, heads):
@@ -341,56 +413,99 @@
 
 
 def shifted(block, axis, distance):
-    devices = range(lax.axis_size(axis))
-    route = [((i - distance) % len(devices), i) for i in devices]
-    return lax.ppermute(block, axis, route)
-
-
-def forward(field, dim, axis):
-    arrived = shifted(lax.slice_in_dim(field, 0, SHIFT, axis=dim), axis, -1)
-    return jnp.concatenate([lax.slice_in_dim(field, SHIFT, None, axis=dim), arrived], dim)
-
-
-def backward(field, dim, axis):
-    edge = field.shape[dim] - SHIFT
-    arrived = shifted(lax.slice_in_dim(field, edge, None, axis=dim), axis, 1)
-    return jnp.concatenate([arrived, lax.slice_in_dim(field, 0, edge, axis=dim)], dim)
+    count = lax.axis_size(axis)
+    return lax.ppermute(block, axis, [((i - distance) % count, i) for i in range(count)])
+
+
+def crossed(block, axis, bit):
+    return lax.ppermute(block, axis, [(i, i ^ bit) for i in range(lax.axis_size(axis))])
+
+
+def sum_everywhere(value, axes):
+    sizes = {axis: lax.axis_size(axis) for axis in axes}
+    if any(size & (size - 1) for size in sizes.values()) or sizes[axes[1]] < 2:
+        return lax.psum(value, axes)
+    near = axes[1]
+    bit = lax.axis_index(near) & 1
+    size = value.shape[0] // 2
+    keep = lax.dynamic_slice_in_dim(value, bit * size, size, 0)
+    send = lax.dynamic_slice_in_dim(value, (1 - bit) * size, size, 0)
+    part = keep + crossed(send, near, 1)
+    for axis in (axes[2], axes[1], axes[0]):
+        step = 2 if axis == near else 1
+        while step < sizes[axis]:
+            part = part + crossed(part, axis, step)
+            step *= 2
+    other = crossed(part, near, 1)
+    upper = bit == 1
+    return jnp.concatenate([jnp.where(upper, other, part), jnp.where(upper, part, other)], 0)
+
+
+def both(first, second):
+    pad = jnp.zeros(first.shape[:3] + (128 - first.shape[3],), BF16)
+    return jnp.concatenate([first, pad, second, pad], -1)
+
+
+CHUNKS = (1, 3)
 
 
 def shards(inputs, d_out, layer_norm_gain, layer_norm_bias, w_qkv, b_qkv, w_proj, rel_bias):
     cells_x, cells_y, cells_z, feats = inputs.shape
     heads = rel_bias.shape[0]
-    pad = jnp.zeros(inputs.shape[:3] + (128 - feats,), BF16)
-    xd = jnp.concatenate([inputs, pad, d_out, pad], -1)
-    for dim, axis in enumerate(("gx", "gy", "gz")):
-        xd = forward(xd, dim, axis)
-    deep = cells_z // WIN
-    xd = xd.reshape(cells_x, cells_y, deep, WIN, 256)
-    xd = jnp.pad(xd, ((0, 0), (0, 0), (0, 0), (0, 1), (0, 0))).reshape(cells_x, cells_y, deep * 8, 256)
+    axes = ("gx", "gy", "gz")
+    rows = cells_x // WIN
+    counts = [CHUNKS[0], rows - CHUNKS[0]] if rows > CHUNKS[0] else [rows]
+    bases = [sum(counts[:i]) for i in range(len(counts))]
+
+    def layers(lo, hi, depth):
+        return jnp.concatenate(
+            [both(inputs[lo:hi, SHIFT:, :depth], d_out[lo:hi, SHIFT:, :depth]), yhalo[lo:hi, :, :depth]], 1
+        )
+
+    yhalo = shifted(both(inputs[:, :SHIFT], d_out[:, :SHIFT]), "gy", -1)
+    xhalo = shifted(layers(0, SHIFT, cells_z), "gx", -1)
+    zhalos = []
+    for base, count in zip(bases, counts):
+        lo, hi = WIN * base + SHIFT, WIN * (base + count) + SHIFT
+        edge = layers(lo, min(hi, cells_x), SHIFT)
+        if hi > cells_x:
+            edge = jnp.concatenate([edge, xhalo[:, :, :SHIFT]], 0)
+        zhalos.append(shifted(edge, "gz", -1))
     table = jnp.pad(rel_bias * 1.4426950408889634, ((0, 8 - heads), (0, TABLE - rel_bias.shape[1])))
-    bias = expand_table(table, heads)
+    tables = expand_table(table, heads)
     wside, wtrans = side_weights(w_qkv, b_qkv, heads)
     gain = jnp.broadcast_to(layer_norm_gain[:, None], (feats, LANES))
     shift = jnp.broadcast_to(layer_norm_bias[:, None], (feats, LANES))
-    flags = jnp.stack(
-        [(lax.axis_index(a) == lax.axis_size(a) - 1).astype(F32) for a in ("gx", "gy", "gz")]
-    )
-    d_x, pairs, gq, gkv, gproj, vec = window_call(
-        flags, xd, bias, gain, shift, wside, wtrans, w_proj, w_qkv[:, :feats], w_qkv[:, feats:], heads
-    )
-    d_x = d_x.reshape(cells_x, cells_y, deep, 8, feats)[:, :, :, :WIN].reshape(inputs.shape)
-    for dim, axis in enumerate(("gx", "gy", "gz")):
-        d_x = backward(d_x, dim, axis)
-    rel = fold_table(pairs)[:heads]
-    vec = jnp.sum(vec, -1)
-    both = jnp.concatenate([gq, gkv], 1)
+    weights = (gain, shift, wside, wtrans, w_proj, w_qkv)
+    flags = jnp.stack([(lax.axis_index(a) == lax.axis_size(a) - 1).astype(F32) for a in axes])
+    sums, fields = None, []
+    for at, (base, count) in enumerate(zip(bases, counts)):
+        last = at == len(counts) - 1
+        field, *sums = window_call(
+            base, count, flags, (inputs, d_out), yhalo, zhalos[at], xhalo if last else None, tables, weights,
+            sums, heads,
+        )
+        arrived = shifted(field[:, :, :SHIFT], "gz", 1)
+        fields.append(jnp.concatenate([arrived, field[:, :, SHIFT:cells_z]], 2))
+    total = sum_everywhere(fold_sums(sums), axes)
+    arrived = shifted(fields[-1][-SHIFT:], "gx", 1)
+    d_x = jnp.concatenate([arrived] + fields[:-1] + [fields[-1][:-SHIFT]], 0)
+    edge = cells_y - SHIFT
+    d_x = jnp.concatenate([shifted(d_x[:, edge:], "gy", 1), d_x[:, :edge]], 1)
     count = inputs.shape[0] * inputs.shape[1] * inputs.shape[2]
-    for a in ("gx", "gy", "gz"):
+    for a in axes:
         count *= lax.axis_size(a)
-    totals = lax.psum((both, gproj, rel, vec), ("gx", "gy", "gz"))
-    both, gproj, rel, vec = [t * float(count) ** (-0.5) for t in totals]
+    total = total * float(count) ** (-0.5)
+    per_head = TABLE // LANES
+    rel = total[REL_AT : REL_AT + heads * per_head].reshape(heads, TABLE)
     return (
-        d_x, both[:feats], both[feats], gproj, rel[:, : rel_bias.shape[1]], vec[0], vec[1],
+        d_x,
+        total[:feats, : 3 * feats],
+        total[feats, : 3 * feats],
+        total[:feats, 3 * feats :],
+        rel[:, : rel_bias.shape[1]],
+        total[feats + 1, :feats],
+        total[feats + 2, :feats],
     )
 
 

time: 349 us -> 161 us (0.46)
  waiting for transfers between devices: 138 us -> 23.8 us
  blocking collectives: 38.5 us -> 0 us
  other arithmetic: 26.2 us -> 6.65 us
  between operations: 14.3 us -> 1.15 us
  local copies, waits for them, and re-layouts: 33.1 us -> 22.5 us
  Pallas kernels: 84.3 us -> 93 us
    psum x1 -> x0, waiting for transfers between devices: 111 us -> none  [shards(): totals = lax.psum((both, gproj, rel, vec), ('gx', 'gy', 'gz'))]
    psum x1 -> x0, blocking collectives: 38.5 us -> none  [shards(): totals = lax.psum((both, gproj, rel, vec), ('gx', 'gy', 'gz'))]
    concatenate x8 -> x5, other arithmetic: 12.9 us -> 3.92 us  [the longest x1 2.08 us: shards(): d_x = jnp.concatenate([shifted(d_x[:, edge:], 'gy', 1), d_x[:, :edge]], 1)]
    pallas_call x3 -> x4, Pallas kernels: 84.3 us -> 93 us  [the longest x2 78.3 us: window_call(): pl.pallas_call(functools.partial(window_body, base, xhalo is not None, su...]
    concatenate x5, local copies, waits for them, and re-layouts: 6.88 us -> 1.06 us  [side_weights(): jnp.concatenate([w_qkv] + [p[None] for p in parts] + [jnp.zeros((128 - fe...]
    ppermute x6 -> x14, waiting for transfers between devices: 27.3 us -> 23.8 us  [the longest x6 20.7 us: crossed(): lax.ppermute(block, axis, [(i, i ^ bit) for i in range(lax.axis_size(axis...]
    slice x12 -> x23, local copies, waits for them, and re-layouts: 10 us -> 12.6 us  [the longest x3 3.28 us: layers(): d_out[lo:hi, SHIFT:, :depth]]
    ppermute x6 -> x14, starting transfers between devices: 12.4 us -> 13.5 us  [the longest x8 11.7 us: shifted(): lax.ppermute(block, axis, [((i - distance) % count, i) for i in range(cou...]
  transfers between devices with their start and end apart: 7 -> 14, of which waited for: 5 -> 7; matrix products, arithmetic and copies ran while one was open for 11% -> 12% of each run, Pallas kernels for 2% -> 23%
where the time goes in v2:
time: 161 us
  Pallas kernels  93 us (58%)
  waiting for transfers between devices  23.8 us (15%)
  local copies, waits for them, and re-layouts  22.5 us (14%)
  starting transfers between devices  13.5 us (8%)
  other arithmetic  6.65 us (4%)
    pallas_call x2, Pallas kernels, window_call(): pl.pallas_call(functools.partial(window_body, base, xhalo is not None, su...  78.3 us
    ppermute x6, waiting for transfers between devices, crossed(): lax.ppermute(block, axis, [(i, i ^ bit) for i in range(lax.axis_size(axis...  20.7 us
    ppermute x8, starting transfers between devices, shifted(): lax.ppermute(block, axis, [((i - distance) % count, i) for i in range(cou...  11.7 us
    pallas_call x1, Pallas kernels, expand_table(): pl.pallas_call(expand_body, out_shape=[jax.ShapeDtypeStruct((heads, ROWS,...  8.08 us
    pallas_call x1, Pallas kernels, fold_sums(): pl.pallas_call(fold_body, out_shape=jax.ShapeDtypeStruct((128, LANES), F3...  6.62 us
    slice x3, local copies, waits for them, and re-layouts, layers(): d_out[lo:hi, SHIFT:, :depth]  3.28 us
    slice x3, local copies, waits for them, and re-layouts, layers(): inputs[lo:hi, SHIFT:, :depth]  3.27 us
  transfers between devices with their start and end apart: 14, of which 7 were waited for; matrix products, arithmetic and copies ran while one was open for 12% of the time, Pallas kernels for 23%

profile of v2, /device:TPU:0, one launch (start us, length us, event | category | flops | bytes accessed | tf_op | source)
XLA Modules:
  0.0 160.6 jit_solution(2087136775976893635)
XLA Ops:
  0.7 1.0 slice.91
  1.6 0.9 slice.92
  2.6 0.3 pad_maximum_fusion.5
  2.9 2.5 %collective-permute-start = (bf16[28,3,7,256]{3,2,1,0:T(8,128)(2,1)S(1)}, bf16[28,3,7,256]{3,2,1,0:T(8,128)(2,1)S(1)}, u32[]{:S(2)}, u32[]{:S(2)}) collective-permute-start(bf16[28,3,7,256]{3,2,1,0:T(8,128)(2,1)S(1)} %pad_maximum_fusion.5), channel_id=1, source_target_pairs={{2,0},{4,2},{6,4},{0,6},{3,1},{5,3},{7,5},{1,7},{10,8},{12,10},{14... | collective-permute-start | bytes 903176 | tf_op jit(solution)/shard_map/ppermute | solution.py:417
  7.1 0.6 pad.4.table_ref
  7.7 8.1 %expand.1 = (f32[3,344,384]{2,1,0:T(8,128)}, bf16[384,392]{1,0:T(8,128)(2,1)}, bf16[392,384]{1,0:T(8,128)(2,1)}, f32[344,128]{1,0:T(8,128)}, bf16[16,384]{1,0:T(8,128)(2,1)}) custom-call(f32[8,2304]{1,0:T(8,128)} %pad.4.table_ref), custom_call_target="tpu_custom_call" | custom-call | flops 4000000000 | bytes 2000000 | tf_op jit(solution)/shard_map/expand/pallas_call | solution.py:123
  15.9 1.0 slice.103
  16.9 1.0 slice.104
  17.9 0.9 slice.96
  18.9 0.9 slice.97
  20.3 3.8 %collective-permute-start.1 = (bf16[3,28,7,256]{3,2,1,0:T(8,128)(2,1)S(1)}, bf16[3,28,7,256]{3,2,1,0:T(8,128)(2,1)S(1)}, u32[]{:S(2)}, u32[]{:S(2)}) collective-permute-start(bf16[3,28,7,256]{3,2,1,0:T(8,128)(2,1)S(1)} %pad_maximum_fusion.6), channel_id=1, source_target_pairs={{8,0},{16,8},{24,16},{0,24},{9,1},{17,9},{25,17},{1,25},{10,2},{18... | collective-permute-start | bytes 903176 | tf_op jit(solution)/shard_map/ppermute | solution.py:417
  24.2 0.6 pad_maximum_fusion.4
  24.8 1.6 collective-permute-start.3
  26.4 0.7 pad_maximum_fusion.8.refs_13_.refs_14_
  27.1 1.3 slice.93
  28.4 1.3 slice.94
  29.7 0.9 copy.43.refs_12_.refs_13_
  30.8 0.4 collective-permute-done.1.refs_5_
  31.4 0.7 pad_maximum_fusion.3
  32.1 1.6 collective-permute-start.2
  33.7 0.6 add_convert_fusion.refs_0_
  34.3 2.7 %collective-permute-done.3.refs_4_ = bf16[7,28,3,256]{3,2,1,0:T(4,128)(2,1)S(1)} collective-permute-done((bf16[7,28,3,256]{3,2,1,0:T(4,128)(2,1)S(1)}, bf16[7,28,3,256]{3,2,1,0:T(4,128)(2,1)S(1)}, u32[]{:S(2)}, u32[]{:S(2)}) %collective-permute-start.3) | collective-permute-done | bytes 301088 | tf_op jit(solution)/shard_map/ppermute | solution.py:417
  37.1 0.8 broadcast_in_dim.51.refs_10_.refs_11_
  37.9 0.7 broadcast_in_dim.52.refs_11_.refs_12_
  38.6 21.5 %windows.2 = (bf16[7,28,8,96]{3,2,1,0:T(8,128)(2,1)}, f32[3,344,384]{2,1,0:T(8,128)}, f32[112,96]{1,0:T(8,128)}, f32[112,192]{1,0:T(8,128)}, f32[96,96]{1,0:T(8,128)}, /*index=5*/f32[2,96,384]{2,1,0:T(8,128)}) custom-call(f32[3]{0:T(128)} %add_convert_fusion.refs_0_, bf16[28,28,7,96]{3,2,1,0:T(8,128)(2,1)} %refs_1_.3, bf16[28,28,7,96]{3,2,1,0:T(8,128)(2,1)} %refs_2_.3, ...), custom_call_target="tpu_custom_call" | custom-call | flops 8800000000 | bytes 8000000 | tf_op jit(solution)/shard_map/windows/pallas_call | solution.py:368
  60.1 1.9 %copy.42.refs_4_ = bf16[21,28,3,256]{3,2,1,0:T(4,128)(2,1)} copy(bf16[21,28,3,256]{3,1,2,0:T(8,128)(2,1)S(1)} %collective-permute-done.2) | data formatting | bytes 1806336 | tf_op jit(solution)/shard_map/ppermute | solution.py:417
  62.0 56.8 %windows.3 = (bf16[21,28,8,96]{3,2,1,0:T(8,128)(2,1)}, f32[3,344,384]{2,1,0:T(8,128)}, f32[112,96]{1,0:T(8,128)}, f32[112,192]{1,0:T(8,128)}, f32[96,96]{1,0:T(8,128)}, /*index=5*/f32[2,96,384]{2,1,0:T(8,128)}) custom-call(f32[3]{0:T(128)} %add_convert_fusion.refs_0_, bf16[28,28,7,96]{3,2,1,0:T(8,128)(2,1)} %refs_1_.3, bf16[28,28,7,96]{3,2,1,0:T(8,128)(2,1)} %refs_2_.3, ...), custom_call_target="tpu_custom_call" | custom-call | flops 26400000000 | bytes 8000000 | tf_op jit(solution)/shard_map/windows/pallas_call | solution.py:368
  118.8 1.4 slice.106
  120.3 1.6 collective-permute-start.4
  121.9 6.6 %fold.1 = f32[128,384]{1,0:T(8,128)} custom-call(f32[3,344,384]{2,1,0:T(8,128)} %get-tuple-element.36.pairs_ref, f32[112,96]{1,0:T(8,128)} %get-tuple-element.37.gq_ref, f32[112,192]{1,0:T(8,128)} %get-tuple-element.38.gkv_ref, f32[96,96]{1,0:T(8,128)} %get-tuple-element.39.gproj_ref, f32[2,96,384]{2,1,0:T(8,128)} %get-tuple-element.40.vec_ref), custom_call_target="tpu_custom_call" | custom-call | flops 3000000000 | bytes 2000000 | tf_op jit(solution)/shard_map/fold/pallas_call | solution.py:177
  128.6 1.5 constant_dynamic-slice_fusion
  130.2 0.6 collective-permute-start.6
  130.7 0.3 slice.107
  131.1 0.7 collective-permute-done.8
  131.7 0.9 dynamic-slice_add_fusion
  132.7 0.9 collective-permute-start.9
  133.6 0.3 copy.45
  134.1 5.6 %collective-permute-done.9 = f32[64,384]{1,0:T(8,128)S(1)} collective-permute-done((f32[64,384]{1,0:T(8,128)S(1)}, f32[64,384]{1,0:T(8,128)S(1)}, u32[]{:S(2)}, u32[]{:S(2)}) %collective-permute-start.9) | collective-permute-done | bytes 98336 | tf_op jit(solution)/shard_map/ppermute | solution.py:421
  139.8 0.6 collective-permute-start.10
  140.5 3.9 %collective-permute-done.10 = f32[64,384]{1,0:T(8,128)S(1)} collective-permute-done((f32[64,384]{1,0:T(8,128)S(1)}, f32[64,384]{1,0:T(8,128)S(1)}, u32[]{:S(2)}, u32[]{:S(2)}) %collective-permute-start.10) | collective-permute-done | bytes 98336 | tf_op jit(solution)/shard_map/ppermute | solution.py:421
  144.7 4.4 %collective-permute-done.11 = f32[64,384]{1,0:T(8,128)S(1)} collective-permute-done((f32[64,384]{1,0:T(8,128)S(1)}, f32[64,384]{1,0:T(8,128)S(1)}, u32[]{:S(2)}, u32[]{:S(2)}) %collective-permute-start.11) | collective-permute-done | bytes 98336 | tf_op jit(solution)/shard_map/ppermute | solution.py:421
  149.2 6.0 %collective-permute-done.12 = f32[64,384]{1,0:T(8,128)S(1)} collective-permute-done((f32[64,384]{1,0:T(8,128)S(1)}, f32[64,384]{1,0:T(8,128)S(1)}, u32[]{:S(2)}, u32[]{:S(2)}) %collective-permute-start.12) | collective-permute-done | bytes 98336 | tf_op jit(solution)/shard_map/ppermute | solution.py:421
  155.3 2.1 %fusion.1 = bf16[28,28,7,96]{3,2,1,0:T(8,128)(2,1)} fusion(bf16[21,28,4,96]{3,2,1,0:T(4,128)(2,1)S(1)} %slice.107, bf16[21,28,3,96]{3,2,1,0:T(4,128)(2,1)S(1)} %copy.45, bf16[3,28,7,96]{3,2,1,0:T(8,128)(2,1)S(1)} %collective-permute-done.5, bf16[7,28,4,96]{3,2,1,0:T(4,128)(2,1)S(1)} %slice.110, bf16[7,28,3,96]{3,2,1,0:T(4,128)(2,1)S(1)} %collective-permute-done.6, ...), kind=kLoop, calls=%fused_computation.2 | loop fusion | flops 6322176 | bytes 2333184 | tf_op jit(solution)/shard_map/concatenate | solution.py:494
  157.5 0.7 slice.128
  158.1 0.7 slice.130
  158.8 0.6 slice_reduce_fusion
  159.4 0.5 slice_bitcast_fusion.2
  159.9 0.6 reshape.80
  (84 shorter events, 3.5 us)
Async XLA Ops:
  0.6 4.8 %copy-start.7 = (f32[288]{0:T(512)S(1)}, f32[288]{0:T(512)}, u32[]{:S(2)}) copy-start(f32[288]{0:T(512)} %param.13) | copy-start | bytes 3460
  0.6 5.8 %copy-start.5 = (bf16[96,288]{1,0:T(8,128)(2,1)S(1)}, bf16[96,288]{1,0:T(8,128)(2,1)}, u32[]{:S(2)}) copy-start(bf16[96,288]{1,0:T(8,128)(2,1)} %refs_16_.1) | copy-start | bytes 165892
  1.6 5.4 %copy-start.6 = (f32[3,2197]{1,0:T(4,128)S(1)}, f32[3,2197]{1,0:T(4,128)}, u32[]{:S(2)}) copy-start(f32[3,2197]{1,0:T(4,128)} %param.15) | copy-start | bytes 79096
  2.9 17.1 %collective-permute-start = (bf16[28,3,7,256]{3,2,1,0:T(8,128)(2,1)S(1)}, bf16[28,3,7,256]{3,2,1,0:T(8,128)(2,1)S(1)}, u32[]{:S(2)}, u32[]{:S(2)}) collective-permute-start(bf16[28,3,7,256]{3,2,1,0:T(8,128)(2,1)S(1)} %pad_maximum_fusion.5), channel_id=1, source_target_pairs={{2,0},{4,2},{6,4},{0,6},{3,1},{5,3},{7,5},{1,7},{10,8},{12,10},{14... | collective-permute-start | bytes 903176 | tf_op jit(solution)/shard_map/ppermute | solution.py:417
  20.0 10.7 %copy-start.3 = (bf16[28,3,7,256]{3,2,1,0:T(8,128)(2,1)}, bf16[28,3,7,256]{3,2,1,0:T(8,128)(2,1)S(1)}, u32[]{:S(2)}) copy-start(bf16[28,3,7,256]{3,2,1,0:T(8,128)(2,1)S(1)} %collective-permute-done.refs_3_) | copy-start | bytes 903172
  20.3 10.9 %collective-permute-start.1 = (bf16[3,28,7,256]{3,2,1,0:T(8,128)(2,1)S(1)}, bf16[3,28,7,256]{3,2,1,0:T(8,128)(2,1)S(1)}, u32[]{:S(2)}, u32[]{:S(2)}) collective-permute-start(bf16[3,28,7,256]{3,2,1,0:T(8,128)(2,1)S(1)} %pad_maximum_fusion.6), channel_id=1, source_target_pairs={{8,0},{16,8},{24,16},{0,24},{9,1},{17,9},{25,17},{1,25},{10,2},{18... | collective-permute-start | bytes 903176 | tf_op jit(solution)/shard_map/ppermute | solution.py:417
  24.8 12.2 %collective-permute-start.3 = (bf16[7,28,3,256]{3,2,1,0:T(4,128)(2,1)S(1)}, bf16[7,28,3,256]{3,2,1,0:T(4,128)(2,1)S(1)}, u32[]{:S(2)}, u32[]{:S(2)}) collective-permute-start(bf16[7,28,3,256]{3,2,1,0:T(4,128)(2,1)S(1)} %pad_maximum_fusion.4), channel_id=1, source_target_pairs={{1,0},{0,1},{3,2},{2,3},{5,4},{4,5},{7,6},{6,7},{9,8},{8,9},{11,10... | collective-permute-start | bytes 903176 | tf_op jit(solution)/shard_map/ppermute | solution.py:417
  31.2 0.9 copy-start.4
  31.3 5.8 %copy-start.8 = (f32[96]{0:T(128)S(1)}, f32[96]{0:T(128)}, u32[]{:S(2)}) copy-start(f32[96]{0:T(128)} %param.10) | copy-start | bytes 1156
  31.3 6.6 %copy-start.9 = (f32[96]{0:T(128)S(1)}, f32[96]{0:T(128)}, u32[]{:S(2)}) copy-start(f32[96]{0:T(128)} %param.11) | copy-start | bytes 1156
  32.1 28.0 %collective-permute-start.2 = (bf16[21,28,3,256]{3,1,2,0:T(8,128)(2,1)S(1)}, bf16[21,28,3,256]{3,1,2,0:T(8,128)(2,1)S(1)}, u32[]{:S(2)}, u32[]{:S(2)}) collective-permute-start(bf16[21,28,3,256]{3,1,2,0:T(8,128)(2,1)S(1)} %pad_maximum_fusion.3), channel_id=1, source_target_pairs={{1,0},{0,1},{3,2},{2,3},{5,4},{4,5},{7,6},{6,7},{9,8},{8,9},{11,10... | collective-permute-start | bytes 2709512 | tf_op jit(solution)/shard_map/ppermute | solution.py:417
  37.1 1.5 copy-start.10
  120.3 13.2 %collective-permute-start.4 = (bf16[21,28,3,96]{3,1,2,0:T(8,128)(2,1)S(1)}, bf16[21,28,3,96]{3,1,2,0:T(8,128)(2,1)S(1)}, u32[]{:S(2)}, u32[]{:S(2)}) collective-permute-start(bf16[21,28,3,96]{3,1,2,0:T(8,128)(2,1)S(1)} %copy.44), channel_id=1, source_target_pairs={{1,0},{0,1},{3,2},{2,3},{5,4},{4,5},{7,6},{6,7},{9,8},{8,9},{11,10... | collective-permute-start | bytes 1016072 | tf_op jit(solution)/shard_map/ppermute | solution.py:417
  121.9 8.2 %copy-start.1 = (bf16[7,28,8,96]{3,2,1,0:T(8,128)(2,1)S(1)}, bf16[7,28,8,96]{3,2,1,0:T(8,128)(2,1)}, u32[]{:S(2)}) copy-start(bf16[7,28,8,96]{3,2,1,0:T(8,128)(2,1)} %get-tuple-element.35) | copy-start | bytes 903172
  121.9 8.8 %copy-start = (bf16[21,28,8,96]{3,2,1,0:T(8,128)(2,1)S(1)}, bf16[21,28,8,96]{3,2,1,0:T(8,128)(2,1)}, u32[]{:S(2)}) copy-start(bf16[21,28,8,96]{3,2,1,0:T(8,128)(2,1)} %get-tuple-element.34) | copy-start | bytes 2709508
  130.1 1.6 %collective-permute-start.8 = (f32[64,384]{1,0:T(8,128)}, f32[64,384]{1,0:T(8,128)}, u32[]{:S(2)}, u32[]{:S(2)}) collective-permute-start(f32[64,384]{1,0:T(8,128)} %constant_dynamic-slice_fusion), channel_id=1, source_target_pairs={{0,2},{2,0},{4,6},{6,4},{1,3},{3,1},{5,7},{7,5},{8,10},{10,8},{12,... | collective-permute-start | bytes 294920 | tf_op jit(solution)/shard_map/ppermute | solution.py:421
  130.1 1.6 %copy-start.2 = (f32[128,384]{1,0:T(8,128)S(1)}, f32[128,384]{1,0:T(8,128)}, u32[]{:S(2)}) copy-start(f32[128,384]{1,0:T(8,128)} %fold.1) | copy-start | bytes 589828
  130.2 14.4 %collective-permute-start.6 = (bf16[7,28,3,96]{3,2,1,0:T(4,128)(2,1)S(1)}, bf16[7,28,3,96]{3,2,1,0:T(4,128)(2,1)S(1)}, u32[]{:S(2)}, u32[]{:S(2)}) collective-permute-start(bf16[7,28,3,96]{3,2,1,0:T(4,128)(2,1)S(1)} %slice.109), channel_id=1, source_target_pairs={{1,0},{0,1},{3,2},{2,3},{5,4},{4,5},{7,6},{6,7},{9,8},{8,9},{11,10... | collective-permute-start | bytes 338696 | tf_op jit(solution)/shard_map/ppermute | solution.py:417
  132.7 7.1 %collective-permute-start.9 = (f32[64,384]{1,0:T(8,128)S(1)}, f32[64,384]{1,0:T(8,128)S(1)}, u32[]{:S(2)}, u32[]{:S(2)}) collective-permute-start(f32[64,384]{1,0:T(8,128)S(1)} %dynamic-slice_add_fusion), channel_id=1, source_target_pairs={{0,1},{1,0},{2,3},{3,2},{4,5},{5,4},{6,7},{7,6},{8,9},{9,8},{10,11... | collective-permute-start | bytes 294920 | tf_op jit(solution)/shard_map/ppermute | solution.py:421
  134.0 10.5 %collective-permute-start.5 = (bf16[3,28,7,96]{3,2,1,0:T(8,128)(2,1)S(1)}, bf16[3,28,7,96]{3,2,1,0:T(8,128)(2,1)S(1)}, u32[]{:S(2)}, u32[]{:S(2)}) collective-permute-start(bf16[3,28,7,96]{3,2,1,0:T(8,128)(2,1)S(1)} %pad_maximum_fusion.7), channel_id=1, source_target_pairs={{24,0},{0,8},{8,16},{16,24},{25,1},{1,9},{9,17},{17,25},{26,2},{2,... | collective-permute-start | bytes 338696 | tf_op jit(solution)/shard_map/ppermute | solution.py:417
  139.8 4.7 %collective-permute-start.10 = (f32[64,384]{1,0:T(8,128)S(1)}, f32[64,384]{1,0:T(8,128)S(1)}, u32[]{:S(2)}, u32[]{:S(2)}) collective-permute-start(f32[64,384]{1,0:T(8,128)S(1)} %add.26), channel_id=1, source_target_pairs={{0,4},{2,6},{4,0},{6,2},{1,5},{3,7},{5,1},{7,3},{8,12},{10,14},{12... | collective-permute-start | bytes 294920 | tf_op jit(solution)/shard_map/ppermute | solution.py:421
  144.5 4.7 %collective-permute-start.11 = (f32[64,384]{1,0:T(8,128)S(1)}, f32[64,384]{1,0:T(8,128)S(1)}, u32[]{:S(2)}, u32[]{:S(2)}) collective-permute-start(f32[64,384]{1,0:T(8,128)S(1)} %add.27), channel_id=1, source_target_pairs={{0,8},{8,0},{16,24},{24,16},{1,9},{9,1},{17,25},{25,17},{2,10},{10... | collective-permute-start | bytes 294920 | tf_op jit(solution)/shard_map/ppermute | solution.py:421
  144.7 10.7 %collective-permute-start.7 = (bf16[28,3,7,96]{3,2,1,0:T(8,128)(2,1)S(1)}, bf16[28,3,7,96]{3,2,1,0:T(8,128)(2,1)S(1)}, u32[]{:S(2)}, u32[]{:S(2)}) collective-permute-start(bf16[28,3,7,96]{3,2,1,0:T(8,128)(2,1)S(1)} %maximum_maximum_fusion.1), channel_id=1, source_target_pairs={{6,0},{0,2},{2,4},{4,6},{7,1},{1,3},{3,5},{5,7},{14,8},{8,10},{10,... | collective-permute-start | bytes 338696 | tf_op jit(solution)/shard_map/ppermute | solution.py:417
  149.1 6.1 %collective-permute-start.12 = (f32[64,384]{1,0:T(8,128)S(1)}, f32[64,384]{1,0:T(8,128)S(1)}, u32[]{:S(2)}, u32[]{:S(2)}) collective-permute-start(f32[64,384]{1,0:T(8,128)S(1)} %add.28), channel_id=1, source_target_pairs={{0,16},{8,24},{16,0},{24,8},{1,17},{9,25},{17,1},{25,9},{2,18},{10... | collective-permute-start | bytes 294920 | tf_op jit(solution)/shard_map/ppermute | solution.py:421
  155.2 2.2 %collective-permute-start.13 = (f32[64,384]{1,0:T(8,128)S(1)}, f32[64,384]{1,0:T(8,128)S(1)}, u32[]{:S(2)}, u32[]{:S(2)}) collective-permute-start(f32[64,384]{1,0:T(8,128)S(1)} %add.29), channel_id=1, source_target_pairs={{0,2},{2,0},{4,6},{6,4},{1,3},{3,1},{5,7},{7,5},{8,10},{10,8},{12,... | collective-permute-start | bytes 294920 | tf_op jit(solution)/shard_map/ppermute | solution.py:421

commit v3 on v2

--- a/solution.py
+++ b/solution.py
@@ -1,4 +1,5 @@
 import functools
+import itertools
 
 import jax
 import jax.numpy as jnp
@@ -17,7 +18,6 @@
 WIDE = 1152
 TABLE = 2304
 HID = 112
-REL_AT = 104
 AUG = 80
 BIG = 1e30
 F32 = jnp.float32
@@ -78,7 +78,45 @@
     return jnp.where((place & 7) == 7, -1, (place >> 3) * WIN + third)
 
 
-def expand_body(table_ref, bias_ref, pack_ref, unpack_ref, kmask_ref, qmask_ref, base_ref, ones_ref, wide_ref):
+CUT, LOW, HIGH = 256, 896, 768
+
+
+def weight_tables(wqkv_ref, bqkv_ref, wside_ref, wtrans_ref, heads):
+    feats = wqkv_ref.shape[0]
+    hdim = feats // heads
+    rows = [part.astype(F32) for part in thirds(bqkv_ref[...])]
+    full = jnp.concatenate(
+        [wqkv_ref[...].astype(F32)] + rows + [jnp.zeros((128 - feats - 3, 3 * feats), F32)], 0
+    )
+    pad = jnp.zeros((128, 128 - 2 * hdim), F32)
+    for part in range(2):
+        for head in range(heads):
+            lo = feats * (part + 1) + hdim * head
+            piece = full[:, lo : lo + hdim]
+            at = 128 * (part * heads + head)
+            wside_ref[:, at : at + 128] = jnp.concatenate([piece, piece, pad], 1).astype(BF16)
+    turned = jnp.concatenate([full, jnp.zeros((128, LANES - 3 * feats), F32)], 1).T[:, :HID]
+    row = lax.broadcasted_iota(jnp.int32, (16, HID), 0)
+    lane = lax.broadcasted_iota(jnp.int32, (16, HID), 1)
+    one = jnp.where((row == 0) & (lane == feats), 1.0, 0.0).astype(BF16)
+    for head in range(heads):
+        lo = 2 * feats + hdim * head
+        wtrans_ref[48 * head : 48 * head + hdim] = turned[lo : lo + hdim].astype(BF16)
+        wtrans_ref[48 * head + hdim : 48 * head + 48] = one
+    wtrans_ref[48 * heads :] = turned[: 2 * feats].astype(BF16)
+
+
+def expand_body(
+    table_ref, wqkv_ref, bqkv_ref, gain_ref, shift_ref,
+    bias_ref, pack_ref, unpack_ref, kmask_ref, qmask_ref, wside_ref, wtrans_ref, gains_ref, shifts_ref,
+    base_ref, ones_ref, wide_ref,
+):
+    weight_tables(wqkv_ref, bqkv_ref, wside_ref, wtrans_ref, bias_ref.shape[0])
+    for source, target in ((gain_ref, gains_ref), (shift_ref, shifts_ref)):
+        turned = jnp.broadcast_to(source[...], (128, source.shape[1]))
+        turned = jnp.concatenate([turned, jnp.zeros((128, 128 - source.shape[1]), F32)], 1).T
+        for part in range(LANES // 128):
+            target[:, 128 * part : 128 * part + 128] = turned[: source.shape[1]]
     place = lax.broadcasted_iota(jnp.int32, (LANES, SLAB), 1)
     token = lax.broadcasted_iota(jnp.int32, (LANES, SLAB), 0)
     pack_ref[...] = jnp.where(token == slab_token(place), 1.0, 0.0).astype(BF16)
@@ -113,13 +151,19 @@
                 rows = 8 * (first * WIN + second)
                 wide_ref[rows : rows + 8, :] = base_ref[:, at : at + WIDE]
         high, mid, low = thirds(wide_ref[...])
-        full = (dot(high, ones_ref[...]) + dot(mid, ones_ref[...])) + dot(low, ones_ref[...])
+        full = [
+            (dot(high[:, a:b], ones_ref[a:b, c:d]) + dot(mid[:, a:b], ones_ref[a:b, c:d]))
+            + dot(low[:, a:b], ones_ref[a:b, c:d])
+            for a, b, c, d in ((0, LOW, 0, CUT), (HIGH, WIDE, CUT, LANES))
+        ]
+        full = jnp.concatenate(full, 1)
         for group in range(WIN * WIN):
             bias_ref[head, WIN * group : WIN * group + WIN, :] = full[8 * group : 8 * group + WIN]
         bias_ref[head, TOK:ROWS, :] = jnp.zeros((ROWS - TOK, LANES), F32)
 
 
-def expand_table(table, heads, interpret=False):
+def expand_table(table, w_qkv, b_qkv, gain, shift, heads, interpret=False):
+    feats = w_qkv.shape[0]
     return pl.pallas_call(
         expand_body,
         out_shape=[
@@ -128,6 +172,10 @@
             jax.ShapeDtypeStruct((SLAB, LANES), BF16),
             jax.ShapeDtypeStruct((ROWS, 128), F32),
             jax.ShapeDtypeStruct((16, LANES), BF16),
+            jax.ShapeDtypeStruct((128, 2 * heads * 128), BF16),
+            jax.ShapeDtypeStruct((48 * heads + 2 * feats, HID), BF16),
+            jax.ShapeDtypeStruct((feats, LANES), F32),
+            jax.ShapeDtypeStruct((feats, LANES), F32),
         ],
         scratch_shapes=[
             pltpu.VMEM((8, TABLE), F32),
@@ -135,9 +183,10 @@
             pltpu.VMEM((SLAB, WIDE), F32),
         ],
         cost_estimate=pl.CostEstimate(flops=4_000_000_000, bytes_accessed=2_000_000, transcendentals=0),
+        compiler_params=pltpu.CompilerParams(vmem_limit_bytes=24 * 1024 * 1024),
         interpret=interpret,
         name="expand",
-    )(table)
+    )(table, w_qkv, b_qkv[None], gain[None], shift[None])
 
 
 def column_sums(value):
@@ -146,50 +195,119 @@
     return jnp.sum(part.T, 0, keepdims=True)
 
 
-def fold_body(pairs_ref, gq_ref, gkv_ref, gproj_ref, vec_ref, out_ref, rows_ref, ones_ref, total_ref):
+def fold_body(bit_ref, pairs_ref, gq_ref, gkv_ref, gproj_ref, vec_ref, keep_ref, send_ref, out_ref,
+              all_ref, rows_ref, ones_ref, total_ref):
+    feats = gproj_ref.shape[0]
+    proj = jnp.concatenate([gproj_ref[...], jnp.zeros((HID - feats, feats), F32)], 0)
+    all_ref[...] = jnp.concatenate([gq_ref[...], gkv_ref[...], proj], 1)
+    for at in range(2):
+        all_ref[feats + 1 + at : feats + 2 + at, :128] = column_sums(vec_ref[at])
+    upper = bit_ref[0] == 1
+    half = HID // 2
+    keep_ref[...] = jnp.where(upper, all_ref[half:], all_ref[:half])
+    send_ref[...] = jnp.where(upper, all_ref[:half], all_ref[half:])
     ones_ref[...] = spread_ones()
     heads = pairs_ref.shape[0]
-    feats = gproj_ref.shape[0]
     out_ref[...] = jnp.zeros(out_ref.shape, F32)
-    proj = jnp.concatenate([gproj_ref[...], jnp.zeros((8, feats), F32)], 0)
-    out_ref[:REL_AT, :] = jnp.concatenate([gq_ref[:REL_AT], gkv_ref[:REL_AT], proj], 1)
-    for at in range(2):
-        out_ref[feats + 1 + at : feats + 2 + at, :128] = column_sums(vec_ref[at])
     rows_ref[...] = jnp.zeros(rows_ref.shape, F32)
     for head in range(heads):
         for group in range(WIN * WIN):
-            rows_ref[8 * group : 8 * group + WIN, :] = pairs_ref[head, WIN * group : WIN * group + WIN, :]
-        high, low = halves(rows_ref[...])
-        wide = dot(high, ones_ref[...], NT) + dot(low, ones_ref[...], NT)
-        total_ref[...] = jnp.zeros(total_ref.shape, F32)
+            rows_ref[head, 8 * group : 8 * group + WIN, :] = pairs_ref[head, WIN * group : WIN * group + WIN, :]
+    for head in range(heads):
+        high, low = halves(rows_ref[head])
+        wide, rest = [
+            dot(high[:, c:d], ones_ref[a:b, c:d], NT) + dot(low[:, c:d], ones_ref[a:b, c:d], NT)
+            for a, b, c, d in ((0, LOW, 0, CUT), (HIGH, WIDE, CUT, LANES))
+        ]
+        wide = jnp.concatenate([wide[:, :HIGH], wide[:, HIGH:] + rest[:, : LOW - HIGH], rest[:, LOW - HIGH :]], 1)
+        total_ref[head] = jnp.zeros(total_ref.shape[1:], F32)
         for first in range(WIN):
             for second in range(WIN):
                 at = offset_of(first, second)
                 rows = 8 * (first * WIN + second)
-                total_ref[:, at : at + WIDE] = total_ref[:, at : at + WIDE] + wide[rows : rows + 8]
-        entries = jnp.sum(shear(total_ref[...], 1), 0, keepdims=True)
+                total_ref[head, :, at : at + WIDE] = total_ref[head, :, at : at + WIDE] + wide[rows : rows + 8]
+        entries = jnp.sum(shear(total_ref[head], 1), 0, keepdims=True)
         for part in range(TABLE // LANES):
-            row = REL_AT + head * (TABLE // LANES) + part
+            row = head * (TABLE // LANES) + part
             out_ref[row : row + 1, :] = entries[:, LANES * part : LANES * part + LANES]
 
 
-def fold_sums(sums, interpret=False):
+def fold_sums(bit, sums):
+    heads = sums[0].shape[0]
+    rows = -(-heads * (TABLE // LANES) // 8) * 8
+    half = jax.ShapeDtypeStruct((HID // 2, LANES), F32)
     return pl.pallas_call(
         fold_body,
-        out_shape=jax.ShapeDtypeStruct((128, LANES), F32),
+        in_specs=[pl.BlockSpec(memory_space=pltpu.SMEM)] + [pl.BlockSpec(memory_space=pltpu.VMEM)] * 5,
+        out_shape=[half, half, jax.ShapeDtypeStruct((rows, LANES), F32)],
         scratch_shapes=[
-            pltpu.VMEM((SLAB, LANES), F32),
+            pltpu.VMEM((HID, LANES), F32),
+            pltpu.VMEM((heads, SLAB, LANES), F32),
             pltpu.VMEM((WIDE, LANES), BF16),
-            pltpu.VMEM((8, TABLE), F32),
+            pltpu.VMEM((heads, 8, TABLE), F32),
         ],
         cost_estimate=pl.CostEstimate(flops=3_000_000_000, bytes_accessed=2_000_000, transcendentals=0),
-        interpret=interpret,
+        compiler_params=pltpu.CompilerParams(vmem_limit_bytes=24 * 1024 * 1024),
         name="fold",
-    )(*sums)
-
-
-def gather(x_ref, d_ref, yhalo_ref, xhalo_ref, zhalo_ref, block_ref, base, last):
+    )(bit, *sums)
+
+
+def join_body(x_ref, d_ref, field_ref):
     feats = x_ref.shape[3]
+    zero = jnp.zeros(field_ref.shape[:3] + (128 - feats,), BF16)
+    field_ref[:, :, :, :128] = jnp.concatenate([x_ref[...], zero], -1)
+    field_ref[:, :, :, 128:] = jnp.concatenate([d_ref[...], zero], -1)
+
+
+def join_fields(inputs, d_out):
+    rows = WIN if inputs.shape[0] % WIN == 0 else inputs.shape[0]
+    block = (rows,) + inputs.shape[1:]
+    spec = pl.BlockSpec(block, lambda i: (i, 0, 0, 0))
+    return pl.pallas_call(
+        join_body,
+        grid=(inputs.shape[0] // rows,),
+        in_specs=[spec, spec],
+        out_specs=pl.BlockSpec(block[:3] + (256,), lambda i: (i, 0, 0, 0)),
+        out_shape=jax.ShapeDtypeStruct(inputs.shape[:3] + (256,), BF16),
+        compiler_params=pltpu.CompilerParams(vmem_limit_bytes=20 * 1024 * 1024),
+        cost_estimate=pl.CostEstimate(flops=1_000_000_000, bytes_accessed=6_000_000, transcendentals=0),
+        name="join",
+    )(inputs, d_out)
+
+
+def split_body(factor, bit_ref, part_ref, other_ref, entries_ref, gq_ref, gb_ref, gproj_ref, grel_ref, gain_ref, shift_ref):
+    feats = gproj_ref.shape[0]
+    wide = gq_ref.shape[1]
+    upper = bit_ref[0] == 1
+    low = jnp.where(upper, other_ref[...], part_ref[...])
+    high = jnp.where(upper, part_ref[...], other_ref[...])
+    full = jnp.concatenate([low, high], 0) * factor
+    gq_ref[...] = full[:feats, :wide]
+    gb_ref[...] = full[feats : feats + 1, :wide]
+    gproj_ref[...] = full[:feats, wide:]
+    gain_ref[...] = full[feats + 1 : feats + 2, :feats]
+    shift_ref[...] = full[feats + 2 : feats + 3, :feats]
+    per_head = TABLE // LANES
+    for head in range(grel_ref.shape[0]):
+        for part in range(per_head):
+            lo = LANES * part
+            hi = min(lo + LANES, grel_ref.shape[1])
+            row = head * per_head + part
+            grel_ref[head : head + 1, lo:hi] = entries_ref[row : row + 1, : hi - lo] * factor
+
+
+def split_sums(factor, bit, part, other, entries, feats, heads, count):
+    shapes = [(feats, 3 * feats), (1, 3 * feats), (feats, feats), (heads, count), (1, feats), (1, feats)]
+    return pl.pallas_call(
+        functools.partial(split_body, factor),
+        in_specs=[pl.BlockSpec(memory_space=pltpu.SMEM)] + [pl.BlockSpec(memory_space=pltpu.VMEM)] * 3,
+        out_shape=[jax.ShapeDtypeStruct(shape, F32) for shape in shapes],
+        cost_estimate=pl.CostEstimate(flops=500_000_000, bytes_accessed=500_000, transcendentals=0),
+        name="split",
+    )(bit, part, other, entries)
+
+
+def gather(field_ref, yhalo_ref, xhalo_ref, zhalo_ref, block_ref, base, last):
     row, col = pl.program_id(0), pl.program_id(1)
     at_x = WIN * (row + base) + SHIFT
     at_y = WIN * col + SHIFT
@@ -198,9 +316,7 @@
 
     def own(first, count_x, second, count_y):
         spot = (pl.ds(at_x + first, count_x), pl.ds(at_y + second, count_y))
-        here = (slice(first, first + count_x), slice(second, second + count_y), slice(0, WIN))
-        block_ref[here + (slice(0, feats),)] = x_ref[spot].astype(F32)
-        block_ref[here + (slice(128, 128 + feats),)] = d_ref[spot].astype(F32)
+        block_ref[first : first + count_x, second : second + count_y, :WIN, :] = field_ref[spot].astype(F32)
 
     def arrived(first, count_x):
         block_ref[first : first + count_x, edge:, :WIN, :] = yhalo_ref[pl.ds(at_x + first, count_x)].astype(F32)
@@ -235,11 +351,11 @@
 
 def window_body(base, has_xhalo, has_sums, *refs):
     refs = list(refs)
-    flag_ref, x_ref, d_ref, yhalo_ref, zhalo_ref = refs[:5]
-    refs = refs[5:]
+    flag_ref, field_ref, yhalo_ref, zhalo_ref = refs[:4]
+    refs = refs[4:]
     xhalo_ref = refs.pop(0) if has_xhalo else None
-    bias_ref, pack_ref, unpack_ref, kmask_ref, qmask_ref = refs[:5]
-    gain_ref, shift_ref, wside_ref, wtrans_ref, wproj_ref, wqkv_ref = refs[5:11]
+    bias_ref, pack_ref, unpack_ref, kmask_ref, qmask_ref, wside_ref, wtrans_ref, gain_ref, shift_ref = refs[:9]
+    wproj_ref, wqkv_ref = refs[9:11]
     refs = refs[11:]
     before = [refs.pop(0) for _ in range(5)] if has_sums else None
     dx_ref, pair_ref, gq_ref, gkv_ref, gproj_ref, vec_ref = refs[:6]
@@ -263,7 +379,7 @@
         for ref in (block_ref, qdiag_ref, odiag_ref):
             ref[...] = jnp.zeros(ref.shape, ref.dtype)
 
-    gather(x_ref, d_ref, yhalo_ref, xhalo_ref, zhalo_ref, block_ref, base, last)
+    gather(field_ref, yhalo_ref, xhalo_ref, zhalo_ref, block_ref, base, last)
     block = block_ref[...].reshape(SLAB, 256).astype(BF16)
     packed = dot(pack_ref[...], block)
     dy_tok = packed[:, 128:].astype(BF16)
@@ -301,24 +417,28 @@
     do_t = dot(wproj_ref[...], dy_tok[:, :feats], NT).astype(BF16).astype(F32)
     scaled = q_t.astype(F32) * (scale * 1.4426950408889634)
 
-    for head in range(heads):
-        lo, hi = hdim * head, hdim * (head + 1)
-        span = slice(LANES * head, LANES * (head + 1))
-        q_high, q_low = halves(scaled[lo:hi])
+    spans = [slice(LANES * head, LANES * (head + 1)) for head in range(heads)]
+    parts = [slice(hdim * head, hdim * (head + 1)) for head in range(heads)]
+    tops, o_augs = [], []
+    for head in range(heads):
+        q_high, q_low = halves(scaled[parts[head]])
         q_aug = jnp.concatenate([q_high, q_low, qmask_ref[...]], 0)
         score = dot(kaug_ref[head, :, :AUG], q_aug) + bias_ref[head]
-        score_ref[...] = score
-        top = jnp.max(score, 0, keepdims=True)
-        expo = jnp.exp2(score_ref[...] - top).astype(BF16)
-        expo_ref[:, span] = expo
+        score_ref[head] = score
+        tops.append(jnp.max(score, 0, keepdims=True))
+    for head in range(heads):
+        expo = jnp.exp2(score_ref[head] - tops[head]).astype(BF16)
+        expo_ref[:, spans[head]] = expo
         v_t = turned[48 * head : 48 * head + 48].astype(BF16)
-        out = dot(v_t[:, :ROWS], expo_ref[:, span])
+        out = dot(v_t[:, :ROWS], expo_ref[:, spans[head]])
         inverse = 1.0 / out[hdim : hdim + 1]
         out = out[:hdim] * inverse
-        attn_ref[lo:hi, :] = out.astype(BF16)
-        grad_out = do_t[lo:hi]
+        attn_ref[parts[head], :] = out.astype(BF16)
+        grad_out = do_t[parts[head]]
         mean = jnp.sum(out * grad_out, 0, keepdims=True) * (-inverse)
         o_high, o_low = halves(grad_out * inverse)
+        odiag_ref[parts[head], spans[head]] = o_high
+        qdiag_ref[parts[head], spans[head]] = q_t[parts[head]]
         m_high, m_mid, m_low = thirds(mean)
         row16 = lax.broadcasted_iota(jnp.int32, (16, LANES), 0)
         m_rows = jnp.where(
@@ -326,16 +446,16 @@
             m_high.astype(F32),
             jnp.where(row16 == 1, m_mid.astype(F32), jnp.where(row16 == 2, m_low.astype(F32), 0.0)),
         ).astype(BF16)
-        o_aug = jnp.concatenate([o_high, o_low, m_rows], 0)
-        grads = dot(vaug_ref[head, :, :AUG], o_aug) * expo_ref[:, span].astype(F32)
+        o_augs.append(jnp.concatenate([o_high, o_low, m_rows], 0))
+    dv = dot(expo_ref[...], odiag_ref[...], NT).astype(BF16)
+    for head in range(heads):
+        grads = dot(vaug_ref[head, :, :AUG], o_augs[head]) * expo_ref[:, spans[head]].astype(F32)
         pair_ref[head] = pair_ref[head] + grads
-        grad_ref[:, span] = grads.astype(BF16)
-        qdiag_ref[lo:hi, span] = q_t[lo:hi]
-        odiag_ref[lo:hi, span] = o_high
-        dq_ref[lo:hi, :] = (dot(k_t[lo:hi, :ROWS], grad_ref[:, span]) * scale).astype(BF16)
+        grad_ref[:, spans[head]] = grads.astype(BF16)
+    for head in range(heads):
+        dq_ref[parts[head], :] = (dot(k_t[parts[head], :ROWS], grad_ref[:, spans[head]]) * scale).astype(BF16)
 
     dk = (dot(grad_ref[...], qdiag_ref[...], NT) * scale).astype(BF16)
-    dv = dot(expo_ref[...], odiag_ref[...], NT).astype(BF16)
     dkv = jnp.concatenate([dk, dv], 1)
     dq = dq_ref[...]
     gq_ref[...] = gq_ref[...] + dot(norm_t, dq, NT)
@@ -353,15 +473,14 @@
     dx_ref[...] = spread.reshape(WIN, WIN, 8, feats).astype(BF16)
 
 
-def window_call(base, count, flags, own, yhalo, zhalo, xhalo, tables, weights, sums, heads, interpret=False):
-    cells_x, cells_y, cells_z, feats = own[0].shape
+def window_call(base, count, flags, field, yhalo, zhalo, xhalo, tables, weights, sums, heads, interpret=False):
+    cells_y, feats = field.shape[1], weights[0].shape[0]
     grid = (count, cells_y // WIN)
 
-    def whole(array):
-        zeros = (0,) * array.ndim
-        return pl.BlockSpec(array.shape, lambda *_: zeros)
-
-    arrays = list(own) + [yhalo, zhalo] + ([] if xhalo is None else [xhalo])
+    def whole(_):
+        return pl.BlockSpec(memory_space=pltpu.VMEM)
+
+    arrays = [field, yhalo, zhalo] + ([] if xhalo is None else [xhalo])
     arrays += list(tables) + list(weights) + ([] if sums is None else list(sums))
     shapes = [(heads, ROWS, LANES), (HID, feats), (HID, 2 * feats), (feats, feats), (2, feats, LANES)]
     shapes = [jax.ShapeDtypeStruct(shape, F32) for shape in shapes]
@@ -373,7 +492,7 @@
         out_shape=[jax.ShapeDtypeStruct((WIN * count, cells_y, 8, feats), BF16)] + shapes,
         scratch_shapes=[
             pltpu.VMEM((WIN, WIN, 8, 256), F32),
-            pltpu.VMEM((ROWS, LANES), F32),
+            pltpu.VMEM((heads, ROWS, LANES), F32),
             pltpu.VMEM((ROWS, heads * LANES), BF16),
             pltpu.VMEM((ROWS, heads * LANES), BF16),
             pltpu.VMEM((feats, heads * LANES), BF16),
@@ -384,7 +503,7 @@
             pltpu.VMEM((feats, LANES), BF16),
         ],
         compiler_params=pltpu.CompilerParams(
-            dimension_semantics=("arbitrary",) * 2, vmem_limit_bytes=56 * 1024 * 1024
+            dimension_semantics=("arbitrary",) * 2, vmem_limit_bytes=32 * 1024 * 1024
         ),
         cost_estimate=pl.CostEstimate(
             flops=2_200_000_000 * count * grid[1], bytes_accessed=8_000_000, transcendentals=0
@@ -394,59 +513,45 @@
     )(flags, *arrays)
 
 
-def side_weights(w_qkv, b_qkv, heads):
-    feats = w_qkv.shape[0]
-    hdim = feats // heads
-    parts = thirds(b_qkv)
-    full = jnp.concatenate(
-        [w_qkv] + [p[None] for p in parts] + [jnp.zeros((128 - feats - 3, 3 * feats), BF16)], 0
-    )
-    cols = full.reshape(128, 3, heads, hdim)
-    pad = jnp.zeros((128, 2, heads, 128 - 2 * hdim), BF16)
-    wside = jnp.concatenate([cols[:, 1:], cols[:, 1:], pad], -1).reshape(128, 2 * heads * 128)
-    v_rows = cols[:HID, 2].transpose(1, 2, 0)
-    one = (jnp.arange(HID)[None, None, :] == feats) & (jnp.arange(16)[None, :, None] == 0)
-    one = jnp.broadcast_to(one.astype(BF16), (heads, 16, HID))
-    v_rows = jnp.concatenate([v_rows, one], 1).reshape(48 * heads, HID)
-    qk_rows = full[:HID, : 2 * feats].T
-    return wside, jnp.concatenate([v_rows, qk_rows], 0)
-
-
 def shifted(block, axis, distance):
     count = lax.axis_size(axis)
     return lax.ppermute(block, axis, [((i - distance) % count, i) for i in range(count)])
 
 
-def crossed(block, axis, bit):
-    return lax.ppermute(block, axis, [(i, i ^ bit) for i in range(lax.axis_size(axis))])
-
-
-def sum_everywhere(value, axes):
-    sizes = {axis: lax.axis_size(axis) for axis in axes}
-    if any(size & (size - 1) for size in sizes.values()) or sizes[axes[1]] < 2:
-        return lax.psum(value, axes)
-    near = axes[1]
-    bit = lax.axis_index(near) & 1
-    size = value.shape[0] // 2
-    keep = lax.dynamic_slice_in_dim(value, bit * size, size, 0)
-    send = lax.dynamic_slice_in_dim(value, (1 - bit) * size, size, 0)
-    part = keep + crossed(send, near, 1)
+def crossed(block, axes, masks):
+    sizes = [lax.axis_size(axis) for axis in axes]
+    route = []
+    for place in itertools.product(*map(range, sizes)):
+        other = [at ^ masks.get(axis, 0) for at, axis in zip(place, axes)]
+        source = target = 0
+        for size, at, to in zip(sizes, place, other):
+            source, target = source * size + at, target * size + to
+        route.append((source, target))
+    return lax.ppermute(block, axes, route)
+
+
+def exchanged(part, axes):
+    bits = []
     for axis in (axes[2], axes[1], axes[0]):
-        step = 2 if axis == near else 1
-        while step < sizes[axis]:
-            part = part + crossed(part, axis, step)
+        size = lax.axis_size(axis)
+        if size & (size - 1):
+            part = lax.psum(part, axis)
+            continue
+        step = 2 if axis == axes[1] else 1
+        while step < size:
+            bits.append((axis, step))
             step *= 2
-    other = crossed(part, near, 1)
-    upper = bit == 1
-    return jnp.concatenate([jnp.where(upper, other, part), jnp.where(upper, part, other)], 0)
-
-
-def both(first, second):
-    pad = jnp.zeros(first.shape[:3] + (128 - first.shape[3],), BF16)
-    return jnp.concatenate([first, pad, second, pad], -1)
-
-
-CHUNKS = (1, 3)
+    while bits:
+        one = bits.pop(0)
+        if not bits:
+            part = part + crossed(part, axes, dict([one]))
+            break
+        two = bits.pop(0)
+        joined = {one[0]: one[1]}
+        joined[two[0]] = joined.get(two[0], 0) + two[1]
+        near, far, both = (crossed(part, axes, masks) for masks in (dict([one]), dict([two]), joined))
+        part = (part + near) + (far + both)
+    return part
 
 
 def shards(inputs, d_out, layer_norm_gain, layer_norm_bias, w_qkv, b_qkv, w_proj, rel_bias):
@@ -454,40 +559,57 @@
     heads = rel_bias.shape[0]
     axes = ("gx", "gy", "gz")
     rows = cells_x // WIN
-    counts = [CHUNKS[0], rows - CHUNKS[0]] if rows > CHUNKS[0] else [rows]
+    counts = [1, rows - 2, 1] if rows > 2 else [rows]
     bases = [sum(counts[:i]) for i in range(len(counts))]
 
+    field = join_fields(inputs, d_out)
+    direct = shifted(field[SHIFT : WIN + SHIFT, SHIFT:, :SHIFT], "gz", -1)
+    yhalo = shifted(field[:, :SHIFT], "gy", -1)
+
     def layers(lo, hi, depth):
-        return jnp.concatenate(
-            [both(inputs[lo:hi, SHIFT:, :depth], d_out[lo:hi, SHIFT:, :depth]), yhalo[lo:hi, :, :depth]], 1
-        )
-
-    yhalo = shifted(both(inputs[:, :SHIFT], d_out[:, :SHIFT]), "gy", -1)
-    xhalo = shifted(layers(0, SHIFT, cells_z), "gx", -1)
+        return jnp.concatenate([field[lo:hi, SHIFT:, :depth], yhalo[lo:hi, :, :depth]], 1)
+
+    lo, hi = SHIFT, WIN * counts[0] + SHIFT
     zhalos = []
-    for base, count in zip(bases, counts):
+    xsend = layers(0, SHIFT, cells_z)
+    if hi <= cells_x:
+        corner = yhalo[lo:hi, :, :SHIFT]
+        corner, xsend, rel_bias = lax.optimization_barrier((corner, xsend, rel_bias))
+        zhalos.append(jnp.concatenate([direct, shifted(corner, "gz", -1)], 1))
+    xhalo = shifted(xsend, "gx", -1)
+    table = jnp.pad(rel_bias * 1.4426950408889634, ((0, 8 - heads), (0, TABLE - rel_bias.shape[1])))
+    tables = list(expand_table(table, w_qkv, b_qkv, layer_norm_gain, layer_norm_bias, heads))
+    for base, count in list(zip(bases, counts))[len(zhalos) :]:
         lo, hi = WIN * base + SHIFT, WIN * (base + count) + SHIFT
         edge = layers(lo, min(hi, cells_x), SHIFT)
         if hi > cells_x:
             edge = jnp.concatenate([edge, xhalo[:, :, :SHIFT]], 0)
         zhalos.append(shifted(edge, "gz", -1))
-    table = jnp.pad(rel_bias * 1.4426950408889634, ((0, 8 - heads), (0, TABLE - rel_bias.shape[1])))
-    tables = expand_table(table, heads)
-    wside, wtrans = side_weights(w_qkv, b_qkv, heads)
-    gain = jnp.broadcast_to(layer_norm_gain[:, None], (feats, LANES))
-    shift = jnp.broadcast_to(layer_norm_bias[:, None], (feats, LANES))
-    weights = (gain, shift, wside, wtrans, w_proj, w_qkv)
+    weights = (w_proj, w_qkv)
     flags = jnp.stack([(lax.axis_index(a) == lax.axis_size(a) - 1).astype(F32) for a in axes])
     sums, fields = None, []
     for at, (base, count) in enumerate(zip(bases, counts)):
         last = at == len(counts) - 1
-        field, *sums = window_call(
-            base, count, flags, (inputs, d_out), yhalo, zhalos[at], xhalo if last else None, tables, weights,
+        part, *sums = window_call(
+            base, count, flags, field, yhalo, zhalos[at], xhalo if last else None, tables, weights,
             sums, heads,
         )
-        arrived = shifted(field[:, :, :SHIFT], "gz", 1)
-        fields.append(jnp.concatenate([arrived, field[:, :, SHIFT:cells_z]], 2))
-    total = sum_everywhere(fold_sums(sums), axes)
+        edge = part[:, :, :SHIFT]
+        if last:
+            edge, sums[0] = lax.optimization_barrier((edge, sums[0]))
+        arrived = shifted(edge, "gz", 1)
+        fields.append(jnp.concatenate([arrived, part[:, :, SHIFT:cells_z]], 2))
+    paired = lax.axis_size("gy") % 2 == 0
+    bit = lax.axis_index("gy") & 1 if paired else jnp.zeros((), jnp.int32)
+    keep, send, entries = fold_sums(bit.reshape(1), sums)
+    near = {"gy": 1}
+    if not paired:
+        part, other, entries = lax.psum((keep, send, entries), axes)
+    else:
+        part = jnp.concatenate([keep + crossed(send, axes, near), entries + crossed(entries, axes, near)], 0)
+        part = exchanged(part, axes)
+        part, entries = part[: HID // 2], part[HID // 2 :]
+        other = crossed(part, axes, near)
     arrived = shifted(fields[-1][-SHIFT:], "gx", 1)
     d_x = jnp.concatenate([arrived] + fields[:-1] + [fields[-1][:-SHIFT]], 0)
     edge = cells_y - SHIFT
@@ -495,18 +617,10 @@
     count = inputs.shape[0] * inputs.shape[1] * inputs.shape[2]
     for a in axes:
         count *= lax.axis_size(a)
-    total = total * float(count) ** (-0.5)
-    per_head = TABLE // LANES
-    rel = total[REL_AT : REL_AT + heads * per_head].reshape(heads, TABLE)
-    return (
-        d_x,
-        total[:feats, : 3 * feats],
-        total[feats, : 3 * feats],
-        total[:feats, 3 * feats :],
-        rel[:, : rel_bias.shape[1]],
-        total[feats + 1, :feats],
-        total[feats + 2, :feats],
+    g_qkv, g_bias, g_proj, g_rel, g_gain, g_shift = split_sums(
+        float(count) ** (-0.5), bit.reshape(1), part, other, entries, feats, heads, rel_bias.shape[1]
     )
+    return d_x, g_qkv, g_bias.reshape(-1), g_proj, g_rel, g_gain.reshape(-1), g_shift.reshape(-1)
 
 
 def solution(mesh):

time: 161 us -> 126 us (0.78)
  Pallas kernels: 93 us -> 64.9 us
  local copies, waits for them, and re-layouts: 22.5 us -> 10.9 us
  starting transfers between devices: 13.5 us -> 23.1 us
  waiting for transfers between devices: 23.8 us -> 16.2 us
  other arithmetic: 6.65 us -> 9.99 us
    pallas_call x2 -> x3, Pallas kernels: 78.3 us -> 54.9 us  [window_call(): pl.pallas_call(functools.partial(window_body, base, xhalo is not None, su...]
    ppermute x6 -> x9, waiting for transfers between devices: 20.7 us -> 4.25 us  [crossed(): return lax.ppermute(block, axes, route)]
    ppermute x8 -> x11, waiting for transfers between devices: 3.11 us -> 12 us  [shifted(): lax.ppermute(block, axis, [((i - distance) % count, i) for i in range(cou...]
    slice x18 -> x14, local copies, waits for them, and re-layouts: 12.5 us -> 5.41 us  [the longest x3 2.5 us: layers(): field[lo:hi, SHIFT:, :depth]]
    ppermute x6 -> x9, starting transfers between devices: 1.78 us -> 8.81 us  [crossed(): return lax.ppermute(block, axes, route)]
    pallas_call x1, Pallas kernels: 8.08 us -> 3.83 us  [expand_table(): pl.pallas_call(expand_body, out_shape=[jax.ShapeDtypeStruct((heads, ROWS,...]
    unnamed x25 -> x20, local copies, waits for them, and re-layouts: 0.32 us -> 3.49 us
    ppermute x8 -> x11, starting transfers between devices: 11.7 us -> 14.3 us  [shifted(): lax.ppermute(block, axis, [((i - distance) % count, i) for i in range(cou...]
  transfers between devices with their start and end apart: 14 -> 20, of which waited for: 7 -> 6; matrix products, arithmetic and copies ran while one was open for 12% -> 12% of each run, Pallas kernels for 23% -> 35%
where the time goes in v3:
time: 126 us
  Pallas kernels  64.9 us (52%)
  starting transfers between devices  23.1 us (18%)
  waiting for transfers between devices  16.2 us (13%)
  local copies, waits for them, and re-layouts  10.9 us (9%)
  other arithmetic  9.99 us (8%)
    pallas_call x3, Pallas kernels, window_call(): pl.pallas_call(functools.partial(window_body, base, xhalo is not None, su...  54.9 us
    ppermute x11, starting transfers between devices, shifted(): lax.ppermute(block, axis, [((i - distance) % count, i) for i in range(cou...  14.3 us
    ppermute x11, waiting for transfers between devices, shifted(): lax.ppermute(block, axis, [((i - distance) % count, i) for i in range(cou...  12 us
    ppermute x9, starting transfers between devices, crossed(): return lax.ppermute(block, axes, route)  8.81 us
    ppermute x9, waiting for transfers between devices, crossed(): return lax.ppermute(block, axes, route)  4.25 us
    pallas_call x1, Pallas kernels, expand_table(): pl.pallas_call(expand_body, out_shape=[jax.ShapeDtypeStruct((heads, ROWS,...  3.83 us
    unnamed x20, local copies, waits for them, and re-layouts  3.49 us
    concatenate x1, other arithmetic, shards(): d_x = jnp.concatenate([shifted(d_x[:, edge:], 'gy', 1), d_x[:, :edge]], 1)  3.33 us
  transfers between devices with their start and end apart: 20, of which 6 were waited for; matrix products, arithmetic and copies ran while one was open for 12% of the time, Pallas kernels for 35%

profile of v3, /device:TPU:0, one launch (start us, length us, event | category | flops | bytes accessed | tf_op | source)
XLA Modules:
  0.0 126.1 jit_solution(3108435423178419697)
XLA Ops:
  0.6 1.4 %copy-done = bf16[28,28,7,96]{3,2,1,0:T(8,128)(2,1)S(1)} copy-done((bf16[28,28,7,96]{3,2,1,0:T(8,128)(2,1)S(1)}, bf16[28,28,7,96]{3,2,1,0:T(8,128)(2,1)}, u32[]{:S(2)}) %copy-start) | copy-done | bytes 1053720
  2.1 1.4 %copy-done.1 = bf16[28,28,7,96]{3,2,1,0:T(8,128)(2,1)S(1)} copy-done((bf16[28,28,7,96]{3,2,1,0:T(8,128)(2,1)S(1)}, bf16[28,28,7,96]{3,2,1,0:T(8,128)(2,1)}, u32[]{:S(2)}) %copy-start.1) | copy-done | bytes 1053720
  3.5 1.2 join.1.refs_1_
  4.7 0.8 slice.88
  5.4 2.4 %collective-permute-start = (bf16[28,3,7,256]{3,2,1,0:T(8,128)(2,1)}, bf16[28,3,7,256]{3,2,1,0:T(8,128)(2,1)S(1)}, u32[]{:S(2)}, u32[]{:S(2)}) collective-permute-start(bf16[28,3,7,256]{3,2,1,0:T(8,128)(2,1)} %slice.88), channel_id=1, source_target_pairs={{2,0},{4,2},{6,4},{0,6},{3,1},{5,3},{7,5},{1,7},{10,8},{12,10},{14... | collective-permute-start | bytes 903176 | tf_op jit(solution)/shard_map/ppermute | solution.py:518
  7.8 0.8 slice.97
  8.7 1.5 %collective-permute-start.4 = (bf16[7,25,3,256]{3,2,1,0:T(4,128)(2,1)}, bf16[7,25,3,256]{3,2,1,0:T(4,128)(2,1)}, u32[]{:S(2)}, u32[]{:S(2)}) collective-permute-start(bf16[7,25,3,256]{3,2,1,0:T(4,128)(2,1)} %slice.97), channel_id=1, source_target_pairs={{1,0},{0,1},{3,2},{2,3},{5,4},{4,5},{7,6},{6,7},{9,8},{8,9},{11,10... | collective-permute-start | bytes 806408 | tf_op jit(solution)/shard_map/ppermute | solution.py:518
  10.2 0.7 slice.92
  10.9 1.0 slice.95
  12.0 0.7 slice.89
  12.7 1.2 broadcast_in_dim.9.bqkv_ref
  14.0 1.0 pad_maximum_fusion.7
  15.1 0.8 broadcast_multiply_fusion
  15.9 0.6 collective-permute-start.5
  16.5 1.6 %pad_maximum_fusion.4 = bf16[14,28,3,256]{3,2,1,0:T(4,128)(2,1)S(1)} fusion(bf16[14,3,3,256]{3,2,1,0:T(4,128)(2,1)S(1)} %slice.96, bf16[14,25,3,256]{3,2,1,0:T(4,128)(2,1)} %slice.95), kind=kLoop, calls=%fused_computation.7 | loop fusion | flops 301056 | bytes 1204224 | tf_op jit(solution)/shard_map/concatenate | solution.py:570
  18.1 0.1 copy.15
  18.3 1.6 %collective-permute-start.3 = (bf16[14,28,3,256]{3,1,2,0:T(8,128)(2,1)S(1)}, bf16[14,28,3,256]{3,1,2,0:T(8,128)(2,1)S(1)}, u32[]{:S(2)}, u32[]{:S(2)}) collective-permute-start(bf16[14,28,3,256]{3,1,2,0:T(8,128)(2,1)S(1)} %copy.15), channel_id=1, source_target_pairs={{1,0},{0,1},{3,2},{2,3},{5,4},{4,5},{7,6},{6,7},{9,8},{8,9},{11,10... | collective-permute-start | bytes 1806344 | tf_op jit(solution)/shard_map/ppermute | solution.py:518
  19.8 3.6 %collective-permute-start.1 = (bf16[3,28,7,256]{3,2,1,0:T(8,128)(2,1)S(1)}, bf16[3,28,7,256]{3,2,1,0:T(8,128)(2,1)S(1)}, u32[]{:S(2)}, u32[]{:S(2)}) collective-permute-start(bf16[3,28,7,256]{3,2,1,0:T(8,128)(2,1)S(1)} %pad_maximum_fusion.7), channel_id=1, source_target_pairs={{8,0},{16,8},{24,16},{0,24},{9,1},{17,9},{25,17},{1,25},{10,2},{18... | collective-permute-start | bytes 903176 | tf_op jit(solution)/shard_map/ppermute | solution.py:518
  23.5 3.8 %expand.1 = (f32[3,344,384]{2,1,0:T(8,128)S(1)}, bf16[384,392]{1,0:T(8,128)(2,1)S(1)}, bf16[392,384]{1,0:T(8,128)(2,1)S(1)}, f32[344,128]{1,0:T(8,128)S(1)}, bf1...) custom-call(f32[8,2304]{1,0:T(8,128)S(1)} %pad.4.table_ref, ...), custom_call_target="tpu_custom_call" | custom-call | flops 4000000000 | bytes 2000000 | tf_op jit(solution)/shard_map/expand/pallas_call | solution.py:167
  27.4 1.3 pad_maximum_fusion.6.refs_3_
  28.7 14.0 %windows.3 = (bf16[7,28,8,96]{3,2,1,0:T(8,128)(2,1)S(1)}, f32[3,344,384]{2,1,0:T(8,128)S(1)}, f32[112,96]{1,0:T(8,128)S(1)}, f32[112,192]{1,0:T(8,128)S(1)}, f32...) custom-call(f32[3]{0:T(128)S(1)} %add_convert_fusion.refs_0_, bf16[28,28,7,256]{3,2,1,0:T(8,128)(2,1)S(1)} %join.1.refs_1_, ...), custom_call_target="tpu_custom_call" | custom-call | flops 8800000000 | bytes 8000000 | tf_op jit(solution)/shard_map/windows/pallas_call | solution.py:487
  42.8 0.3 pad_maximum_fusion.5
  43.1 0.6 collective-permute-start.2
  43.6 0.5 copy.16.refs_3_
  44.2 26.8 %windows.4 = (bf16[14,28,8,96]{3,2,1,0:T(8,128)(2,1)S(1)}, f32[3,344,384]{2,1,0:T(8,128)S(1)}, f32[112,96]{1,0:T(8,128)S(1)}, f32[112,192]{1,0:T(8,128)S(1)}, f3...) custom-call(f32[3]{0:T(128)S(1)} %add_convert_fusion.refs_0_, bf16[28,28,7,256]{3,2,1,0:T(8,128)(2,1)S(1)} %join.1.refs_1_, ...), custom_call_target="tpu_custom_call" | custom-call | flops 17600000000 | bytes 8000000 | tf_op jit(solution)/shard_map/windows/pallas_call | solution.py:487
  71.0 14.1 %windows.5 = (bf16[7,28,8,96]{3,2,1,0:T(8,128)(2,1)S(1)}, f32[3,344,384]{2,1,0:T(8,128)S(1)}, f32[112,96]{1,0:T(8,128)S(1)}, f32[112,192]{1,0:T(8,128)S(1)}, f32...) custom-call(f32[3]{0:T(128)S(1)} %add_convert_fusion.refs_0_, bf16[28,28,7,256]{3,2,1,0:T(8,128)(2,1)S(1)} %join.1.refs_1_, ...), custom_call_target="tpu_custom_call" | custom-call | flops 8800000000 | bytes 8000000 | tf_op jit(solution)/shard_map/windows/pallas_call | solution.py:487
  85.2 3.3 %fold.1 = (f32[56,384]{1,0:T(8,128)S(1)}, f32[56,384]{1,0:T(8,128)S(1)}, f32[24,384]{1,0:T(8,128)S(1)}) custom-call(s32[1]{0:T(128)} %bitcast.5.bit_ref, f32[3,344,384]{2,1,0:T(8,128)S(1)} %get-tuple-element.75.pairs_ref, f32[112,96]{1,0:T(8,128)S(1)} %get-tuple-element.76.gq_ref, f32[112,192]{1,0:T(8,128)S(1)} %get-tuple-element.77.gkv_ref, ...), custom_call_target="tpu_custom_call" | custom-call | flops 3000000000 | bytes 2000000 | tf_op jit(solution)/shard_map/fold/pallas_call | solution.py:239
  88.5 0.5 collective-permute-start.12
  89.0 1.5 %collective-permute-start.6 = (bf16[7,28,3,96]{3,2,1,0:T(4,128)(2,1)S(1)}, bf16[7,28,3,96]{3,2,1,0:T(4,128)(2,1)S(1)}, u32[]{:S(2)}, u32[]{:S(2)}) collective-permute-start(bf16[7,28,3,96]{3,2,1,0:T(4,128)(2,1)S(1)} %slice.76), channel_id=1, source_target_pairs={{1,0},{0,1},{3,2},{2,3},{5,4},{4,5},{7,6},{6,7},{9,8},{8,9},{11,10... | collective-permute-start | bytes 338696 | tf_op jit(solution)/shard_map/ppermute | solution.py:518
  90.6 0.9 collective-permute-start.13
  91.5 0.6 collective-permute-start.14
  92.1 2.0 %collective-permute-start.15 = (f32[80,384]{1,0:T(8,128)S(1)}, f32[80,384]{1,0:T(8,128)S(1)}, u32[]{:S(2)}, u32[]{:S(2)}) collective-permute-start(f32[80,384]{1,0:T(8,128)S(1)} %pad_maximum_fusion.9), channel_id=1, source_target_pairs={{0,5},{1,4},{2,7},{3,6},{4,1},{5,0},{6,3},{7,2},{8,13},{9,12},{10,... | collective-permute-start | bytes 368648 | tf_op jit(solution)/shard_map/ppermute | solution.py:530
  94.2 0.9 collective-permute-start.8
  95.4 4.2 %collective-permute-done.6 = bf16[7,28,3,96]{3,2,1,0:T(4,128)(2,1)S(1)} collective-permute-done((bf16[7,28,3,96]{3,2,1,0:T(4,128)(2,1)S(1)}, bf16[7,28,3,96]{3,2,1,0:T(4,128)(2,1)S(1)}, u32[]{:S(2)}, u32[]{:S(2)}) %collective-permute-start.6) | collective-permute-done | bytes 112928 | tf_op jit(solution)/shard_map/ppermute | solution.py:518
  99.5 1.5 %collective-permute-start.9 = (bf16[14,28,3,96]{3,2,1,0:T(4,128)(2,1)S(1)}, bf16[14,28,3,96]{3,2,1,0:T(4,128)(2,1)S(1)}, u32[]{:S(2)}, u32[]{:S(2)}) collective-permute-start(bf16[14,28,3,96]{3,2,1,0:T(4,128)(2,1)S(1)} %slice.81), channel_id=1, source_target_pairs={{1,0},{0,1},{3,2},{2,3},{5,4},{4,5},{7,6},{6,7},{9,8},{8,9},{11,10... | collective-permute-start | bytes 677384 | tf_op jit(solution)/shard_map/ppermute | solution.py:518
  101.2 1.0 collective-permute-done.13
  102.3 4.4 %collective-permute-start.17 = (f32[80,384]{1,0:T(8,128)S(1)}, f32[80,384]{1,0:T(8,128)S(1)}, u32[]{:S(2)}, u32[]{:S(2)}) collective-permute-start(f32[80,384]{1,0:T(8,128)S(1)} %add_add_fusion.1), channel_id=1, source_target_pairs={{0,16},{1,17},{2,18},{3,19},{4,20},{5,21},{6,22},{7,23},{8,24},{9,... | collective-permute-start | bytes 368648 | tf_op jit(solution)/shard_map/ppermute | solution.py:530
  106.7 0.2 collective-permute-start.18
  107.0 0.2 slice.82
  107.2 4.0 %collective-permute-done.7 = bf16[3,28,7,96]{3,2,1,0:T(8,128)(2,1)S(1)} collective-permute-done((bf16[3,28,7,96]{3,2,1,0:T(8,128)(2,1)S(1)}, bf16[3,28,7,96]{3,2,1,0:T(8,128)(2,1)S(1)}, u32[]{:S(2)}, u32[]{:S(2)}) %collective-permute-start.7) | collective-permute-done | bytes 112928 | tf_op jit(solution)/shard_map/ppermute | solution.py:518
  111.2 3.0 %collective-permute-done.9 = bf16[14,28,3,96]{3,2,1,0:T(4,128)(2,1)S(1)} collective-permute-done((bf16[14,28,3,96]{3,2,1,0:T(4,128)(2,1)S(1)}, bf16[14,28,3,96]{3,2,1,0:T(4,128)(2,1)S(1)}, u32[]{:S(2)}, u32[]{:S(2)}) %collective-permute-start.9) | collective-permute-done | bytes 225824 | tf_op jit(solution)/shard_map/ppermute | solution.py:518
  114.4 3.2 %collective-permute-done.17 = f32[80,384]{1,0:T(8,128)S(1)} collective-permute-done((f32[80,384]{1,0:T(8,128)S(1)}, f32[80,384]{1,0:T(8,128)S(1)}, u32[]{:S(2)}, u32[]{:S(2)}) %collective-permute-start.17) | collective-permute-done | bytes 122912 | tf_op jit(solution)/shard_map/ppermute | solution.py:530
  117.7 0.6 slice.99.entries_ref
  118.3 0.9 collective-permute-done.10
  119.2 3.3 %fusion.1 = bf16[28,28,7,96]{3,2,1,0:T(8,128)(2,1)} fusion(bf16[7,28,4,96]{3,2,1,0:T(4,128)(2,1)S(1)} %slice.77, bf16[7,28,3,96]{3,2,1,0:T(4,128)(2,1)S(1)} %collective-permute-done.6, bf16[14,28,4,96]{3,2,1,0:T(4,128)(2,1)S(1)} %slice.82, bf16[14,28,3,96]{3,2,1,0:T(4,128)(2,1)S(1)} %collective-permute-done.9, ...), kind=kLoop, calls=%fused_computation.2 | loop fusion | flops 8429568 | bytes 2333184 | tf_op jit(solution)/shard_map/concatenate | solution.py:616
  122.5 0.6 copy-done.9
  123.1 1.6 %split.1 = (f32[96,288]{1,0:T(8,128)}, f32[1,288]{1,0:T(1,128)}, f32[96,96]{1,0:T(8,128)}, f32[3,2197]{1,0:T(4,128)}, f32[1,96]{1,0:T(1,128)}, /*index=5*/f32[1,96]{1,0:T(1,128)}) custom-call(s32[1]{0:T(128)} %bitcast.5.bit_ref, f32[56,384]{1,0:T(8,128)} %copy-done.8, f32[56,384]{1,0:T(8,128)} %copy-done.9, f32[24,384]{1,0:T(8,128)} %slice.99.entries_ref), custom_call_target="tpu_custom_call" | custom-call | flops 500000000 | bytes 500000 | tf_op jit(solution)/shard_map/split/pallas_call | solution.py:301
  124.8 1.3 %reduce = f32[288]{0:T(512)} reduce(f32[1,288]{1,0:T(1,128)} %get-tuple-element.84, f32[]{:T(128)} %constant.24), dimensions={0}, to_apply=%get-tuple-element.84.reduce_sub_computation | reduce | bytes 2308 | tf_op jit(solution)/shard_map/split/pallas_call | solution.py:301
  (56 shorter events, 1.2 us)
Async XLA Ops:
  0.6 1.4 %copy-start = (bf16[28,28,7,96]{3,2,1,0:T(8,128)(2,1)S(1)}, bf16[28,28,7,96]{3,2,1,0:T(8,128)(2,1)}, u32[]{:S(2)}) copy-start(bf16[28,28,7,96]{3,2,1,0:T(8,128)(2,1)} %x_ref.1) | copy-start | bytes 3161092
  2.1 1.4 %copy-start.1 = (bf16[28,28,7,96]{3,2,1,0:T(8,128)(2,1)S(1)}, bf16[28,28,7,96]{3,2,1,0:T(8,128)(2,1)}, u32[]{:S(2)}) copy-start(bf16[28,28,7,96]{3,2,1,0:T(8,128)(2,1)} %d_ref.1) | copy-start | bytes 3161092
  5.4 8.6 %collective-permute-start = (bf16[28,3,7,256]{3,2,1,0:T(8,128)(2,1)}, bf16[28,3,7,256]{3,2,1,0:T(8,128)(2,1)S(1)}, u32[]{:S(2)}, u32[]{:S(2)}) collective-permute-start(bf16[28,3,7,256]{3,2,1,0:T(8,128)(2,1)} %slice.88), channel_id=1, source_target_pairs={{2,0},{4,2},{6,4},{0,6},{3,1},{5,3},{7,5},{1,7},{10,8},{12,10},{14... | collective-permute-start | bytes 903176 | tf_op jit(solution)/shard_map/ppermute | solution.py:518
  8.7 18.7 %collective-permute-start.4 = (bf16[7,25,3,256]{3,2,1,0:T(4,128)(2,1)}, bf16[7,25,3,256]{3,2,1,0:T(4,128)(2,1)}, u32[]{:S(2)}, u32[]{:S(2)}) collective-permute-start(bf16[7,25,3,256]{3,2,1,0:T(4,128)(2,1)} %slice.97), channel_id=1, source_target_pairs={{1,0},{0,1},{3,2},{2,3},{5,4},{4,5},{7,6},{6,7},{9,8},{8,9},{11,10... | collective-permute-start | bytes 806408 | tf_op jit(solution)/shard_map/ppermute | solution.py:518
  13.9 9.5 %copy-start.2 = (f32[1,288]{1,0:T(1,128)S(1)}, f32[1,288]{1,0:T(1,128)}, u32[]{:S(2)}) copy-start(f32[1,288]{1,0:T(1,128)} %broadcast_in_dim.9.bqkv_ref) | copy-start | bytes 3460
  13.9 9.5 %copy-start.3 = (bf16[96,288]{1,0:T(8,128)(2,1)S(1)}, bf16[96,288]{1,0:T(8,128)(2,1)}, u32[]{:S(2)}) copy-start(bf16[96,288]{1,0:T(8,128)(2,1)} %refs_15_.1) | copy-start | bytes 165892
  13.9 9.5 %copy-start.5 = (f32[96]{0:T(128)S(1)}, f32[96]{0:T(128)}, u32[]{:S(2)}) copy-start(f32[96]{0:T(128)} %param.10) | copy-start | bytes 1156
  13.9 9.6 %copy-start.6 = (f32[96]{0:T(128)S(1)}, f32[96]{0:T(128)}, u32[]{:S(2)}) copy-start(f32[96]{0:T(128)} %param.11) | copy-start | bytes 1156
  15.9 11.5 %collective-permute-start.5 = (bf16[7,3,3,256]{3,2,1,0:T(4,128)(2,1)S(1)}, bf16[7,3,3,256]{3,2,1,0:T(4,128)(2,1)S(1)}, u32[]{:S(2)}, u32[]{:S(2)}) collective-permute-start(bf16[7,3,3,256]{3,2,1,0:T(4,128)(2,1)S(1)} %slice.91), channel_id=1, source_target_pairs={{1,0},{0,1},{3,2},{2,3},{5,4},{4,5},{7,6},{6,7},{9,8},{8,9},{11,10... | collective-permute-start | bytes 96776 | tf_op jit(solution)/shard_map/ppermute | solution.py:518
  18.3 25.4 %collective-permute-start.3 = (bf16[14,28,3,256]{3,1,2,0:T(8,128)(2,1)S(1)}, bf16[14,28,3,256]{3,1,2,0:T(8,128)(2,1)S(1)}, u32[]{:S(2)}, u32[]{:S(2)}) collective-permute-start(bf16[14,28,3,256]{3,1,2,0:T(8,128)(2,1)S(1)} %copy.15), channel_id=1, source_target_pairs={{1,0},{0,1},{3,2},{2,3},{5,4},{4,5},{7,6},{6,7},{9,8},{8,9},{11,10... | collective-permute-start | bytes 1806344 | tf_op jit(solution)/shard_map/ppermute | solution.py:518
  19.8 22.9 %collective-permute-start.1 = (bf16[3,28,7,256]{3,2,1,0:T(8,128)(2,1)S(1)}, bf16[3,28,7,256]{3,2,1,0:T(8,128)(2,1)S(1)}, u32[]{:S(2)}, u32[]{:S(2)}) collective-permute-start(bf16[3,28,7,256]{3,2,1,0:T(8,128)(2,1)S(1)} %pad_maximum_fusion.7), channel_id=1, source_target_pairs={{8,0},{16,8},{24,16},{0,24},{9,1},{17,9},{25,17},{1,25},{10,2},{18... | collective-permute-start | bytes 903176 | tf_op jit(solution)/shard_map/ppermute | solution.py:518
  23.5 5.1 %copy-start.4 = (bf16[96,96]{1,0:T(8,128)(2,1)S(1)}, bf16[96,96]{1,0:T(8,128)(2,1)}, u32[]{:S(2)}) copy-start(bf16[96,96]{1,0:T(8,128)(2,1)} %refs_14_.5) | copy-start | bytes 55300
  28.6 14.1 %copy-start.7 = (bf16[4,25,3,256]{3,2,1,0:T(4,128)(2,1)S(1)}, bf16[4,25,3,256]{3,2,1,0:T(4,128)(2,1)}, u32[]{:S(2)}) copy-start(bf16[4,25,3,256]{3,2,1,0:T(4,128)(2,1)} %slice.89) | copy-start | bytes 460804
  43.1 27.9 %collective-permute-start.2 = (bf16[7,28,3,256]{3,2,1,0:T(4,128)(2,1)S(1)}, bf16[7,28,3,256]{3,2,1,0:T(4,128)(2,1)S(1)}, u32[]{:S(2)}, u32[]{:S(2)}) collective-permute-start(bf16[7,28,3,256]{3,2,1,0:T(4,128)(2,1)S(1)} %pad_maximum_fusion.5), channel_id=1, source_target_pairs={{1,0},{0,1},{3,2},{2,3},{5,4},{4,5},{7,6},{6,7},{9,8},{8,9},{11,10... | collective-permute-start | bytes 903176 | tf_op jit(solution)/shard_map/ppermute | solution.py:518
  88.5 2.1 %collective-permute-start.11 = (f32[56,384]{1,0:T(8,128)S(1)}, f32[56,384]{1,0:T(8,128)S(1)}, u32[]{:S(2)}, u32[]{:S(2)}) collective-permute-start(f32[56,384]{1,0:T(8,128)S(1)} %get-tuple-element.81), channel_id=1, source_target_pairs={{0,2},{1,3},{2,0},{3,1},{4,6},{5,7},{6,4},{7,5},{8,10},{9,11},{10,... | collective-permute-start | bytes 258056 | tf_op jit(solution)/shard_map/ppermute | solution.py:530
  88.5 2.0 %collective-permute-start.12 = (f32[24,384]{1,0:T(8,128)S(1)}, f32[24,384]{1,0:T(8,128)S(1)}, u32[]{:S(2)}, u32[]{:S(2)}) collective-permute-start(f32[24,384]{1,0:T(8,128)S(1)} %get-tuple-element.82), channel_id=1, source_target_pairs={{0,2},{1,3},{2,0},{3,1},{4,6},{5,7},{6,4},{7,5},{8,10},{9,11},{10,... | collective-permute-start | bytes 110600 | tf_op jit(solution)/shard_map/ppermute | solution.py:530
  89.0 10.5 %collective-permute-start.6 = (bf16[7,28,3,96]{3,2,1,0:T(4,128)(2,1)S(1)}, bf16[7,28,3,96]{3,2,1,0:T(4,128)(2,1)S(1)}, u32[]{:S(2)}, u32[]{:S(2)}) collective-permute-start(bf16[7,28,3,96]{3,2,1,0:T(4,128)(2,1)S(1)} %slice.76), channel_id=1, source_target_pairs={{1,0},{0,1},{3,2},{2,3},{5,4},{4,5},{7,6},{6,7},{9,8},{8,9},{11,10... | collective-permute-start | bytes 338696 | tf_op jit(solution)/shard_map/ppermute | solution.py:518
  90.6 11.5 %collective-permute-start.13 = (f32[80,384]{1,0:T(8,128)S(1)}, f32[80,384]{1,0:T(8,128)S(1)}, u32[]{:S(2)}, u32[]{:S(2)}) collective-permute-start(f32[80,384]{1,0:T(8,128)S(1)} %pad_maximum_fusion.9), channel_id=1, source_target_pairs={{0,1},{1,0},{2,3},{3,2},{4,5},{5,4},{6,7},{7,6},{8,9},{9,8},{10,11... | collective-permute-start | bytes 368648 | tf_op jit(solution)/shard_map/ppermute | solution.py:530
  91.5 10.6 %collective-permute-start.14 = (f32[80,384]{1,0:T(8,128)S(1)}, f32[80,384]{1,0:T(8,128)S(1)}, u32[]{:S(2)}, u32[]{:S(2)}) collective-permute-start(f32[80,384]{1,0:T(8,128)S(1)} %pad_maximum_fusion.9), channel_id=1, source_target_pairs={{0,4},{1,5},{2,6},{3,7},{4,0},{5,1},{6,2},{7,3},{8,12},{9,13},{10,... | collective-permute-start | bytes 368648 | tf_op jit(solution)/shard_map/ppermute | solution.py:530
  92.1 10.0 %collective-permute-start.15 = (f32[80,384]{1,0:T(8,128)S(1)}, f32[80,384]{1,0:T(8,128)S(1)}, u32[]{:S(2)}, u32[]{:S(2)}) collective-permute-start(f32[80,384]{1,0:T(8,128)S(1)} %pad_maximum_fusion.9), channel_id=1, source_target_pairs={{0,5},{1,4},{2,7},{3,6},{4,1},{5,0},{6,3},{7,2},{8,13},{9,12},{10,... | collective-permute-start | bytes 368648 | tf_op jit(solution)/shard_map/ppermute | solution.py:530
  94.2 12.4 %collective-permute-start.8 = (bf16[7,28,3,96]{3,2,1,0:T(4,128)(2,1)S(1)}, bf16[7,28,3,96]{3,2,1,0:T(4,128)(2,1)S(1)}, u32[]{:S(2)}, u32[]{:S(2)}) collective-permute-start(bf16[7,28,3,96]{3,2,1,0:T(4,128)(2,1)S(1)} %slice.79), channel_id=1, source_target_pairs={{1,0},{0,1},{3,2},{2,3},{5,4},{4,5},{7,6},{6,7},{9,8},{8,9},{11,10... | collective-permute-start | bytes 338696 | tf_op jit(solution)/shard_map/ppermute | solution.py:518
  99.5 14.6 %collective-permute-start.9 = (bf16[14,28,3,96]{3,2,1,0:T(4,128)(2,1)S(1)}, bf16[14,28,3,96]{3,2,1,0:T(4,128)(2,1)S(1)}, u32[]{:S(2)}, u32[]{:S(2)}) collective-permute-start(bf16[14,28,3,96]{3,2,1,0:T(4,128)(2,1)S(1)} %slice.81), channel_id=1, source_target_pairs={{1,0},{0,1},{3,2},{2,3},{5,4},{4,5},{7,6},{6,7},{9,8},{8,9},{11,10... | collective-permute-start | bytes 677384 | tf_op jit(solution)/shard_map/ppermute | solution.py:518
  102.2 9.0 %collective-permute-start.7 = (bf16[3,28,7,96]{3,2,1,0:T(8,128)(2,1)S(1)}, bf16[3,28,7,96]{3,2,1,0:T(8,128)(2,1)S(1)}, u32[]{:S(2)}, u32[]{:S(2)}) collective-permute-start(bf16[3,28,7,96]{3,2,1,0:T(8,128)(2,1)S(1)} %pad_maximum_fusion.8), channel_id=1, source_target_pairs={{24,0},{0,8},{8,16},{16,24},{25,1},{1,9},{9,17},{17,25},{26,2},{2,... | collective-permute-start | bytes 338696 | tf_op jit(solution)/shard_map/ppermute | solution.py:518
  102.2 12.1 %collective-permute-start.16 = (f32[80,384]{1,0:T(8,128)S(1)}, f32[80,384]{1,0:T(8,128)S(1)}, u32[]{:S(2)}, u32[]{:S(2)}) collective-permute-start(f32[80,384]{1,0:T(8,128)S(1)} %add_add_fusion.1), channel_id=1, source_target_pairs={{0,8},{1,9},{2,10},{3,11},{4,12},{5,13},{6,14},{7,15},{8,0},{9,1},... | collective-permute-start | bytes 368648 | tf_op jit(solution)/shard_map/ppermute | solution.py:530
  102.3 15.3 %collective-permute-start.17 = (f32[80,384]{1,0:T(8,128)S(1)}, f32[80,384]{1,0:T(8,128)S(1)}, u32[]{:S(2)}, u32[]{:S(2)}) collective-permute-start(f32[80,384]{1,0:T(8,128)S(1)} %add_add_fusion.1), channel_id=1, source_target_pairs={{0,16},{1,17},{2,18},{3,19},{4,20},{5,21},{6,22},{7,23},{8,24},{9,... | collective-permute-start | bytes 368648 | tf_op jit(solution)/shard_map/ppermute | solution.py:530
  106.7 10.9 %collective-permute-start.18 = (f32[80,384]{1,0:T(8,128)S(1)}, f32[80,384]{1,0:T(8,128)S(1)}, u32[]{:S(2)}, u32[]{:S(2)}) collective-permute-start(f32[80,384]{1,0:T(8,128)S(1)} %add_add_fusion.1), channel_id=1, source_target_pairs={{0,24},{1,25},{2,26},{3,27},{4,28},{5,29},{6,30},{7,31},{8,16},{9,... | collective-permute-start | bytes 368648 | tf_op jit(solution)/shard_map/ppermute | solution.py:530
  114.3 4.9 %collective-permute-start.10 = (bf16[28,3,7,96]{3,2,1,0:T(8,128)(2,1)S(1)}, bf16[28,3,7,96]{3,2,1,0:T(8,128)(2,1)S(1)}, u32[]{:S(2)}, u32[]{:S(2)}) collective-permute-start(bf16[28,3,7,96]{3,2,1,0:T(8,128)(2,1)S(1)} %maximum_maximum_fusion), channel_id=1, source_target_pairs={{6,0},{0,2},{2,4},{4,6},{7,1},{1,3},{3,5},{5,7},{14,8},{8,10},{10,... | collective-permute-start | bytes 338696 | tf_op jit(solution)/shard_map/ppermute | solution.py:518
  117.7 4.8 %copy-start.8 = (f32[56,384]{1,0:T(8,128)}, f32[56,384]{1,0:T(8,128)S(1)}, u32[]{:S(2)}) copy-start(f32[56,384]{1,0:T(8,128)S(1)} %slice.98.part_ref) | copy-start | bytes 258052
  118.3 4.2 %collective-permute-start.19 = (f32[56,384]{1,0:T(8,128)S(1)}, f32[56,384]{1,0:T(8,128)S(1)}, u32[]{:S(2)}, u32[]{:S(2)}) collective-permute-start(f32[56,384]{1,0:T(8,128)S(1)} %slice.98.part_ref), channel_id=1, source_target_pairs={{0,2},{1,3},{2,0},{3,1},{4,6},{5,7},{6,4},{7,5},{8,10},{9,11},{10,... | collective-permute-start | bytes 258056 | tf_op jit(solution)/shard_map/ppermute | solution.py:530
  122.5 0.6 copy-start.9
